TPU v7x, 256 devices: a whole 4x4x8 slice. The times are simulated.
256 devices in a mesh: col: 32 (over z, y), row: 8 (over x, core).
Axes of the slice: x: 4, y: 4, z: 8, core: 2. Of those that a mesh axis runs over, the one named last changes fastest.
Arguments:
- psi_init: float32 [4096, 2, 4096], P('row', None, 'col')
- left_env: float32 [4096, 3, 4096], P('row')
- mpo_tensor: float32 [3, 3, 2, 2], replicated
- right_env: float32 [4096, 3, 4096], P('col')
Outputs:
- output 1: float32 [4], replicated
- output 2: float32 [4], replicated
- output 3: float32 [4096, 2, 4096], P('row', None, 'col')
All inputs are finite; a program needn't handle non-finite values.
Results may differ from a plain program's by a relative error of at most 0.001.
Values sent between devices are 32-bit elements.
A program may use at most 768 MiB of HBM per device.

v0:
```python
import jax
import jax.numpy as jnp
from jax import lax
from jax.sharding import PartitionSpec as P

LANCZOS_STEPS = 4
EXACT_PREC = lax.Precision.HIGHEST


def solution(mesh):
    all_axes = ("row", "col")

    def global_dot(left_vec, right_vec):
        return lax.psum(jnp.sum(left_vec * right_vec), all_axes)

    def local_steps(psi_blk, left_blk, mpo_tensor, right_blk):
        left_cols = lax.all_to_all(left_blk, "row", 2, 0, tiled=True)

        def apply_ham(vec_blk):
            vec_rows = lax.all_gather(vec_blk, "row", axis=0, tiled=True)
            t_one = jnp.einsum("alc,asb->lcsb", left_cols, vec_rows, precision=EXACT_PREC, preferred_element_type=jnp.float32)
            t_two = jnp.einsum("lcsb,lrst->cbrt", t_one, mpo_tensor, precision=EXACT_PREC, preferred_element_type=jnp.float32)
            y_part = jnp.einsum("cbrt,brd->ctd", t_two, right_blk, precision=EXACT_PREC, preferred_element_type=jnp.float32)
            return lax.psum_scatter(y_part, "col", scatter_dimension=2, tiled=True)

        vec_cur = psi_blk / jnp.sqrt(global_dot(psi_blk, psi_blk))
        vec_prev = jnp.zeros_like(vec_cur)
        beta_prev = jnp.zeros((), jnp.float32)
        alpha_list = []
        beta_list = []
        for step_idx in range(LANCZOS_STEPS):
            work_vec = apply_ham(vec_cur)
            alpha_val = global_dot(vec_cur, work_vec)
            work_vec = work_vec - alpha_val * vec_cur - beta_prev * vec_prev
            beta_val = jnp.sqrt(global_dot(work_vec, work_vec))
            vec_prev = vec_cur
            vec_cur = work_vec / beta_val
            beta_prev = beta_val
            alpha_list.append(alpha_val)
            beta_list.append(beta_val)
        return jnp.stack(alpha_list), jnp.stack(beta_list), vec_cur

    return jax.shard_map(local_steps, mesh=mesh, in_specs=(P("row", None, "col"), P("row", None, None), P(), P("col", None, None)), out_specs=(P(), P(), P("row", None, "col")), check_vma=False)
```

profile of v0, /device:TPU:1, one launch (start us, length us, event | category | flops | bytes accessed | tf_op | source)
XLA Modules:
  0.0 2486.3 jit_solution(18432918385011605958)
XLA Ops:
  7.2 35.0 %copy.32 = f32[512,3,4096]{0,1,2:T(4,128)} copy(f32[512,3,4096]{2,0,1:T(8,128)} %param.5) | data formatting | bytes 50331648 | tf_op args[1]
  53.6 430.7 %psum.63 = f32[]{:T(128)} all-reduce(f32[]{:T(128)} %multiply_reduce_fusion.8), channel_id=1, replica_groups=mesh['col'=32,'row'=8] {'row','col'}, use_global_device_ids=true, to_apply=%region_1.0 | all-reduce | flops 1 | bytes 8 | tf_op jit(solution)/shard_map/psum | solution.py:14
  533.9 26.2 %fusion.16 = f32[3,512,2,128,1]{1,3,0,2,4:T(8,128)} fusion(f32[4096,3,512,1]{2,0,1,3:T(8,128)} %bitcast.103, f32[4096,2,128]{0,2,1:T(8,128)} %all-gather.5.cloned.1.call-done), kind=kOutput, calls=%fused_computation.24 | convolution fusion | flops 19327352832 | bytes 30932992 | tf_op jit(solution)/shard_map/alc,asb->lcsb/dot_general | solution.py:21
  566.2 31.1 %convolution_bitcast_fusion.3 = f32[512,2,4096]{0,2,1:T(8,128)} fusion(f32[128,3,4096]{2,0,1:T(8,128)} %param.7, f32[512,128,3,2]{1,2,3,0:T(4,128)S(1)} %convolution_bitcast_fusion.7), kind=kOutput, calls=%fused_computation.3 | convolution fusion | flops 19327352832 | bytes 24641536 | tf_op jit(solution)/shard_map/cbrt,brd->ctd/dot_general | solution.py:23
  597.4 237.1 %reduce-scatter.5.cloned.1.call-done = f32[512,2,128]{0,2,1:T(8,128)} async-done(((f32[512,2,4096]{0,2,1:T(8,128)}), f32[512,2,128]{0,2,1:T(8,128)}) %reduce-scatter.5.cloned.1.call-update) | async-done | bytes 524304 | tf_op jit(solution)/shard_map/reduce_scatter | solution.py:24
  836.3 79.1 %psum.64 = f32[]{:T(128)} all-reduce(f32[]{:T(128)} %multiply_reduce_fusion.7), channel_id=1, replica_groups=mesh['col'=32,'row'=8] {'row','col'}, use_global_device_ids=true, to_apply=%region_4.0 | all-reduce | flops 1 | bytes 8 | tf_op jit(solution)/shard_map/psum | solution.py:14
  917.9 73.4 %psum.65 = f32[]{:T(128)} all-reduce(f32[]{:T(128)} %multiply_reduce_fusion.6), channel_id=1, replica_groups=mesh['col'=32,'row'=8] {'row','col'}, use_global_device_ids=true, to_apply=%region_6.0 | all-reduce | flops 1 | bytes 8 | tf_op jit(solution)/shard_map/psum | solution.py:14
  994.6 31.0 %all-gather.7.cloned.1.call-done = f32[4096,2,128]{0,2,1:T(8,128)} async-done(((f32[512,2,128]{0,2,1:T(8,128)}), f32[4096,2,128]{0,2,1:T(8,128)}) %all-gather.7.cloned.1.call-update) | async-done | bytes 4194320 | tf_op jit(solution)/shard_map/all_gather | solution.py:20
  1025.6 26.4 %fusion.19 = f32[3,512,2,128,1]{1,3,0,2,4:T(8,128)} fusion(f32[4096,3,512,1]{2,0,1,3:T(8,128)} %bitcast.104, f32[4096,2,128]{0,2,1:T(8,128)} %all-gather.7.cloned.1.call-done), kind=kOutput, calls=%fused_computation.25 | convolution fusion | flops 19327352832 | bytes 30932992 | tf_op jit(solution)/shard_map/alc,asb->lcsb/dot_general | solution.py:21
  1058.0 31.2 %convolution_bitcast_fusion.2 = f32[512,2,4096]{0,2,1:T(8,128)} fusion(f32[128,3,4096]{2,0,1:T(8,128)} %param.7, f32[512,128,3,2]{1,2,3,0:T(4,128)S(1)} %convolution_bitcast_fusion.6), kind=kOutput, calls=%fused_computation.2 | convolution fusion | flops 19327352832 | bytes 24641536 | tf_op jit(solution)/shard_map/cbrt,brd->ctd/dot_general | solution.py:23
  1089.3 240.4 %reduce-scatter.7.cloned.1.call-done = f32[512,2,128]{0,2,1:T(8,128)} async-done(((f32[512,2,4096]{0,2,1:T(8,128)}), f32[512,2,128]{0,2,1:T(8,128)}) %reduce-scatter.7.cloned.1.call-update) | async-done | bytes 524304 | tf_op jit(solution)/shard_map/reduce_scatter | solution.py:24
  1331.5 79.2 %psum.66 = f32[]{:T(128)} all-reduce(f32[]{:T(128)} %multiply_reduce_fusion.5), channel_id=1, replica_groups=mesh['col'=32,'row'=8] {'row','col'}, use_global_device_ids=true, to_apply=%region_9.0 | all-reduce | flops 1 | bytes 8 | tf_op jit(solution)/shard_map/psum | solution.py:14
  1413.1 73.4 %psum.67 = f32[]{:T(128)} all-reduce(f32[]{:T(128)} %get-tuple-element.19), channel_id=1, replica_groups=mesh['col'=32,'row'=8] {'row','col'}, use_global_device_ids=true, to_apply=%region_11.0 | all-reduce | flops 1 | bytes 8 | tf_op jit(solution)/shard_map/psum | solution.py:14
  1488.2 30.9 %all-gather.9.cloned.1.call-done = f32[4096,2,128]{0,2,1:T(8,128)} async-done(((f32[512,2,128]{0,2,1:T(8,128)}), f32[4096,2,128]{0,2,1:T(8,128)}) %all-gather.9.cloned.1.call-update) | async-done | bytes 4194320 | tf_op jit(solution)/shard_map/all_gather | solution.py:20
  1551.4 31.1 %convolution_bitcast_fusion.1 = f32[512,2,4096]{0,2,1:T(8,128)} fusion(f32[128,3,4096]{2,0,1:T(8,128)} %param.7, f32[512,128,3,2]{1,2,3,0:T(4,128)S(1)} %convolution_bitcast_fusion.5), kind=kOutput, calls=%fused_computation.1 | convolution fusion | flops 19327352832 | bytes 24641536 | tf_op jit(solution)/shard_map/cbrt,brd->ctd/dot_general | solution.py:23
  1582.6 240.5 %reduce-scatter.9.cloned.1.call-done = f32[512,2,128]{0,2,1:T(8,128)} async-done(((f32[512,2,4096]{0,2,1:T(8,128)}), f32[512,2,128]{0,2,1:T(8,128)}) %reduce-scatter.9.cloned.1.call-update) | async-done | bytes 524304 | tf_op jit(solution)/shard_map/reduce_scatter | solution.py:24
  1825.0 79.1 %psum.68 = f32[]{:T(128)} all-reduce(f32[]{:T(128)} %multiply_reduce_fusion.3), channel_id=1, replica_groups=mesh['col'=32,'row'=8] {'row','col'}, use_global_device_ids=true, to_apply=%region_14.0 | all-reduce | flops 1 | bytes 8 | tf_op jit(solution)/shard_map/psum | solution.py:14
  1906.5 73.5 %psum.69 = f32[]{:T(128)} all-reduce(f32[]{:T(128)} %get-tuple-element.17), channel_id=1, replica_groups=mesh['col'=32,'row'=8] {'row','col'}, use_global_device_ids=true, to_apply=%region_16.0 | all-reduce | flops 1 | bytes 8 | tf_op jit(solution)/shard_map/psum | solution.py:14
  1981.7 31.0 %all-gather.11.cloned.1.call-done = f32[4096,2,128]{0,2,1:T(8,128)} async-done(((f32[512,2,128]{0,2,1:T(8,128)}), f32[4096,2,128]{0,2,1:T(8,128)}) %all-gather.11.cloned.1.call-update) | async-done | bytes 4194320 | tf_op jit(solution)/shard_map/all_gather | solution.py:20
  2012.7 26.4 %fusion.25 = f32[3,512,2,128,1]{1,3,0,2,4:T(8,128)} fusion(f32[4096,3,512,1]{2,0,1,3:T(8,128)} %bitcast.106, f32[4096,2,128]{0,2,1:T(8,128)} %all-gather.11.cloned.1.call-done), kind=kOutput, calls=%fused_computation.27 | convolution fusion | flops 19327352832 | bytes 30932992 | tf_op jit(solution)/shard_map/alc,asb->lcsb/dot_general | solution.py:21
  2045.1 31.2 %convolution_bitcast_fusion = f32[512,2,4096]{0,2,1:T(8,128)} fusion(f32[128,3,4096]{2,0,1:T(8,128)} %param.7, f32[512,128,3,2]{1,2,3,0:T(4,128)S(1)} %convolution_bitcast_fusion.4), kind=kOutput, calls=%fused_computation | convolution fusion | flops 19327352832 | bytes 24641536 | tf_op jit(solution)/shard_map/cbrt,brd->ctd/dot_general | solution.py:23
  2076.3 240.9 %reduce-scatter.11.cloned.1.call-done = f32[512,2,128]{0,2,1:T(8,128)} async-done(((f32[512,2,4096]{0,2,1:T(8,128)}), f32[512,2,128]{0,2,1:T(8,128)}) %reduce-scatter.11.cloned.1.call-update) | async-done | bytes 524304 | tf_op jit(solution)/shard_map/reduce_scatter | solution.py:24
  2319.0 79.3 %psum.70 = f32[]{:T(128)} all-reduce(f32[]{:T(128)} %multiply_reduce_fusion.1), channel_id=1, replica_groups=mesh['col'=32,'row'=8] {'row','col'}, use_global_device_ids=true, to_apply=%region_19.0 | all-reduce | flops 1 | bytes 8 | tf_op jit(solution)/shard_map/psum | solution.py:14
  2400.6 73.2 %psum.71 = f32[]{:T(128)} all-reduce(f32[]{:T(128)} %get-tuple-element.15), channel_id=1, replica_groups=mesh['col'=32,'row'=8] {'row','col'}, use_global_device_ids=true, to_apply=%region_21.0 | all-reduce | flops 1 | bytes 8 | tf_op jit(solution)/shard_map/psum | solution.py:14
  (55 shorter events, 136.9 us)
Async XLA Ops:
  42.2 10.3 copy-start.1
  42.2 444.5 %copy-start.2 = (f32[3,3,2,2]{1,3,2,0:T(2,128)S(1)}, f32[3,3,2,2]{1,3,2,0:T(2,128)}, u32[]{:S(2)}) copy-start(f32[3,3,2,2]{1,3,2,0:T(2,128)} %param.6) | copy-start | bytes 436
  42.2 444.6 %all-to-all-start = ((f32[512,3,4096]{0,1,2:T(4,128)}), f32[512,3,4096]{0,1,2:T(4,128)}, u32[]{:S(2)}, u32[]{:S(2)}) async-start(f32[512,3,4096]{0,1,2:T(4,128)} %copy.32), calls=%async_computation | async-start | bytes 67108864 | tf_op jit(solution)/shard_map/all_to_all | solution.py:17
  52.4 481.5 %all-gather.5.cloned.1.call-start = ((), (), s32[]{:S(2)}) async-start(), calls=%async_computation.5 | async-start | bytes 4718592 | tf_op jit(solution)/shard_map/all_gather | solution.py:20
  486.1 348.4 %reduce-scatter.5.cloned.1.call-start = ((), (), s32[]{:S(2)}) async-start(), calls=%async_computation.6 | async-start | bytes 17301504 | tf_op jit(solution)/shard_map/reduce_scatter | solution.py:24
  597.3 428.3 %all-gather.7.cloned.1.call-start = ((), (), s32[]{:S(2)}) async-start(), calls=%async_computation.7 | async-start | bytes 4718592 | tf_op jit(solution)/shard_map/all_gather | solution.py:20
  994.5 335.2 %reduce-scatter.7.cloned.1.call-start = ((), (), s32[]{:S(2)}) async-start(), calls=%async_computation.8 | async-start | bytes 17301504 | tf_op jit(solution)/shard_map/reduce_scatter | solution.py:24
  1089.2 240.5 %copy-start = (f32[512,2,128]{0,2,1:T(8,128)S(1)}, f32[512,2,128]{0,2,1:T(8,128)}, u32[]{:S(2)}) copy-start(f32[512,2,128]{0,2,1:T(8,128)} %broadcast_divide_fusion.3) | copy-start | bytes 1572868
  1089.2 429.8 %all-gather.9.cloned.1.call-start = ((), (), s32[]{:S(2)}) async-start(), calls=%async_computation.9 | async-start | bytes 4718592 | tf_op jit(solution)/shard_map/all_gather | solution.py:20
  1488.1 335.1 %reduce-scatter.9.cloned.1.call-start = ((), (), s32[]{:S(2)}) async-start(), calls=%async_computation.10 | async-start | bytes 17301504 | tf_op jit(solution)/shard_map/reduce_scatter | solution.py:24
  1582.6 430.1 %all-gather.11.cloned.1.call-start = ((), (), s32[]{:S(2)}) async-start(), calls=%async_computation.11 | async-start | bytes 4718592 | tf_op jit(solution)/shard_map/all_gather | solution.py:20
  1981.6 335.6 %reduce-scatter.11.cloned.1.call-start = ((), (), s32[]{:S(2)}) async-start(), calls=%async_computation.12 | async-start | bytes 17301504 | tf_op jit(solution)/shard_map/reduce_scatter | solution.py:24
Sparse Core Ops, SparseCore 0:
  486.2 30.4 all-gather.4
  597.4 237.0 reduce-scatter.4
  994.7 30.8 all-gather.6
  1089.4 240.3 reduce-scatter.6
  1488.2 30.7 all-gather.8
  1582.7 240.4 reduce-scatter.8
  1981.8 30.8 all-gather.10
  2076.5 240.6 reduce-scatter.10
where the time goes:
time: 2490 us
  waiting for transfers between devices  1050 us (42%)
  blocking collectives  1040 us (42%)
  matrix products  246 us (10%)
  local copies, waits for them, and re-layouts  91.8 us (4%)
  other arithmetic  26.8 us (1%)
    psum x9, blocking collectives, global_dot(): return lax.psum(jnp.sum(left_vec * right_vec), all_axes)  1040 us
    reduce_scatter x4, waiting for transfers between devices, apply_ham(): return lax.psum_scatter(y_part, 'col', scatter_dimension=2, tiled=True)  959 us
    dot_general x4, matrix products, apply_ham(): jnp.einsum('cbrt,brd->ctd', t_two, right_blk, precision=EXACT_PREC, prefe...  125 us
    dot_general x4, matrix products, apply_ham(): jnp.einsum('alc,asb->lcsb', left_cols, vec_rows, precision=EXACT_PREC, pr...  104 us
    all_gather x4, waiting for transfers between devices, apply_ham(): vec_rows = lax.all_gather(vec_blk, 'row', axis=0, tiled=True)  92.9 us
  transfers between devices with their start and end apart: 9, of which 7 were waited for; matrix products, arithmetic and copies ran while one was open for 2% of the time, Pallas kernels for 0%

commit v1 on v0

v1 whole, which is shorter than its diff:
```python
import functools

import jax
import jax.numpy as jnp
from jax import lax
from jax.experimental import pallas as pl
from jax.experimental.pallas import tpu as pltpu
from jax.sharding import PartitionSpec as P

LANCZOS_STEPS = 4
EXACT_PREC = lax.Precision.HIGHEST
MESH = pl.DeviceIdType.MESH
ROWS = 8
PAIR = range(2)
TRIPLE = range(3)
WAYS = (1, -1)
GONE, HERE = True, False


def fold(body, count, unroll=4):
    while count % unroll:
        unroll //= 2

    def trip(i, carry):
        for u in range(unroll):
            body(i * unroll + u)
        return carry

    lax.fori_loop(0, count // unroll, trip, 0)


def lanczos_kernel(
    nz, nx, wa, wb, n0,
    psi_ref, l_hbm, w_ref, r_hbm,
    scal_ref, vout_ref,
    vbuf, lbuf, rbuf, ubuf, tbuf, vv, rd, ps, po, hx, fx, yx, red, sc,
    ag_s, ag_r, rd_s, rd_r, hx_s, hx_r, fx_s, fx_r, yx_s, yx_r,
    ar_s, ar_r, rr_s, rr_r, io_s, io_r, ld_s, credit,
):
    hops = nz // 2
    half = wb // 2
    quart = half // 4
    col, row = lax.axis_index("col"), lax.axis_index("row")
    z, y, x, c = col // 4, col % 4, row // 2, row % 2
    yh, yl, sub = y // 2, ((y + 1) // 2) % 2, y % 2
    own = z * 2 + yh

    def dev(zz=None, yy=None, xx=None, cc=None):
        zz = z if zz is None else zz
        yy = y if yy is None else yy
        xx = x if xx is None else xx
        cc = c if cc is None else cc
        return {"col": zz * 4 + yy, "row": xx * 2 + cc}

    def zat(off):
        return (z + off + 2 * nz) % nz

    sibling = dev(cc=1 - c)
    yl_partner = dev(yy=y + 1 - 2 * sub)
    yh_partner = dev(yy=3 - y)
    x_mate = dev(xx=x + 1 - 2 * (x % 2))
    z_next = {1: dev(zz=zat(1)), -1: dev(zz=zat(-1))}
    x_next = {1: dev(xx=(x + 1) % nx), -1: dev(xx=(x + nx - 1) % nx)}

    def remote(src, dst, send, recv, to):
        return pltpu.make_async_remote_copy(
            src_ref=src, dst_ref=dst, send_sem=send, recv_sem=recv, device_id=to, device_id_type=MESH
        )

    def rows_of(kind, d=0, h=0):
        start, count = (0, n0) if kind == 0 else (n0, wb - n0)
        if h == hops:
            count //= 2
            if d < 0:
                start += count
        return start, count

    def piece(p, s, k, kind, d, h, mid, to):
        start, count = rows_of(kind, d, h)
        at = vbuf.at[p, s, pl.ds(pl.multiple_of(k * wb + start, ROWS), count), :]
        return remote(at, at, ag_s.at[s, mid], ag_r.at[p, s, mid], to)

    def z_id(d, line, h):
        return ((0 if d > 0 else 1) * 3 + line) * hops + h - 1

    def z_copy(p, s, d, line, h, gone):
        k = zat(-d * (h - 1 if gone else h)) * 2 + (1 - yh if line == 2 else yh)
        return piece(p, s, k, min(line, 1), d, h, z_id(d, line, h), z_next[d])

    pair_last = 6 * hops

    def pair_copy(p, s, kind, d, h, gone):
        if kind == 1:
            mid = pair_last
        elif h == 0:
            mid = pair_last + 1
        else:
            mid = pair_last + 2 + (0 if d > 0 else 1) * hops + h - 1
        k = zat(-d * h) * 2 + (yh if gone else 1 - yh)
        return piece(p, s, k, kind, d, h, mid, yh_partner)

    def own_sends(p, s):
        pair_copy(p, s, 1, 0, 0, GONE).start()
        for line in PAIR:
            for d in WAYS:
                z_copy(p, s, d, line, 1, GONE).start()
        pair_copy(p, s, 0, 0, 0, GONE).start()

    def take_pair(p, s):
        pair_copy(p, s, 1, 0, 0, HERE).wait_recv()
        for d in WAYS:
            z_copy(p, s, d, 2, 1, GONE).start()

    def take_hop(p, s, line, h):
        for d in WAYS:
            z_copy(p, s, d, line, h, HERE).wait_recv()
            if h < hops:
                z_copy(p, s, d, line, h + 1, GONE).start()
            if line == 0:
                pair_copy(p, s, 0, d, h, GONE).start()

    def take_cross(p, s, h):
        for d in WAYS if h else (0,):
            pair_copy(p, s, 0, d, h, HERE).wait_recv()

    def drain_sends(p, s):
        pair_copy(p, s, 1, 0, 0, GONE).wait_send()
        pair_copy(p, s, 0, 0, 0, GONE).wait_send()
        for d in WAYS:
            for h in range(1, hops + 1):
                for line in TRIPLE:
                    z_copy(p, s, d, line, h, GONE).wait_send()
                pair_copy(p, s, 0, d, h, GONE).wait_send()

    def events(p, s):
        out = [lambda: take_pair(p, s)]
        for h in range(1, hops + 1):
            for line in TRIPLE:
                out.append(functools.partial(take_hop, p, s, line, h))
        return out

    groups = (
        (0, nx * 2, row, lambda d: {"col": col, "row": (row + d) % (nx * 2)}),
        (nx * 2, 4, y, lambda d: dev(yy=(y + d) % 4)),
        (nx * 2 + 4, nz, z, lambda d: dev(zz=(z + d) % nz)),
    )

    def sum_send(which, stage, tile):
        base, count, me, peer = groups[stage]
        red[which, base + me] = tile
        at = red.at[which, base + me]
        for d in range(1, count):
            remote(at, at, ar_s.at[which, stage], ar_r.at[which, stage], peer(d)).start()

    def sum_take(which, stage):
        base, count, _, _ = groups[stage]
        at = red.at[which, pl.ds(base, count - 1)]
        pltpu.make_async_copy(at, at, ar_r.at[which, stage]).wait()
        pltpu.make_async_copy(at, at, ar_s.at[which, stage]).wait()
        total = red[which, base]
        for i in range(1, count):
            total = total + red[which, base + i]
        return total

    lanes = red.shape[-1]

    def narrow(tile):
        out = tile[:, :lanes]
        for i in range(1, wa // lanes):
            out = out + tile[:, i * lanes : (i + 1) * lanes]
        return out

    def block(i):
        return pl.ds(pl.multiple_of(i * ROWS, ROWS), ROWS)

    def own_block(i):
        return pl.ds(pl.multiple_of(own * wb + i * ROWS, ROWS), ROWS)

    def accumulate(term):
        def trip(i, acc):
            for s in PAIR:
                acc = acc + term(s, i)
            return acc

        return lax.fori_loop(0, wb // ROWS, trip, jnp.zeros((ROWS, wa), jnp.float32), unroll=4)

    def alpha_open(p):
        acc = accumulate(lambda s, i: vv[p, s, block(i), :] * vbuf[p, s, own_block(i), :])
        sum_send(0, 0, narrow(acc))

    def alpha_close(tile, slot):
        value = jnp.full((ROWS, wa), jnp.sum(tile), jnp.float32)
        sc[0] = value
        scal_ref[slot] = value[:, :lanes]

    def beta_open(p):
        alpha, beta = sc[0], sc[2]

        def term(s, i):
            u = vbuf[p, s, own_block(i), :] - alpha * vv[p, s, block(i), :] - beta * vv[1 - p, s, block(i), :]
            vv[1 - p, s, block(i), :] = u
            return u * u

        sum_send(1, 0, narrow(accumulate(term)))

    def beta_close(p, tile, slot):
        value = jnp.sqrt(jnp.full((ROWS, wa), jnp.sum(tile), jnp.float32))
        sc[1] = value
        scal_ref[LANCZOS_STEPS + slot] = value[:, :lanes]

        def scale(i):
            for s in PAIR:
                vv[1 - p, s, block(i), :] = vv[1 - p, s, block(i), :] / value

        fold(scale, wb // ROWS)

    def r_rows(r, of_sub, q):
        return rbuf.at[pl.ds(pl.multiple_of(r * wb + of_sub * half + q * quart, ROWS), quart), :]

    q_own, q_mate = (x % 2) * 2 + c, (1 - x % 2) * 2 + c
    q_sib, q_sib_mate = (x % 2) * 2 + 1 - c, (1 - x % 2) * 2 + 1 - c

    def r_copy(way, r, gone):
        if way == 0:
            src = r_hbm.at[r, pl.ds(pl.multiple_of(q_own * quart, ROWS), quart), :]
            dst = r_rows(r, sub if gone else 1 - sub, q_own)
            return remote(src, dst, rr_s.at[0, r], rr_r.at[0, r], yl_partner)
        if way == 1:
            at = r_rows(r, 1 - sub, q_own if gone else q_mate)
            return remote(at, at, rr_s.at[1, r], rr_r.at[1, r], x_mate)
        if way == 2:
            at = r_rows(r, 1 - sub, q_own if gone else q_sib)
        else:
            at = r_rows(r, 1 - sub, q_mate if gone else q_sib_mate)
        return remote(at, at, rr_s.at[way, r], rr_r.at[way, r], sibling)

    def r_first(r):
        r_copy(0, r, HERE).wait_recv()
        r_copy(1, r, GONE).start()
        r_copy(2, r, GONE).start()

    def r_second(r):
        r_copy(1, r, HERE).wait_recv()
        r_copy(3, r, GONE).start()

    def r_last():
        for r in TRIPLE:
            r_copy(2, r, HERE).wait_recv()
            r_copy(3, r, HERE).wait_recv()
            for way in range(4):
                r_copy(way, r, GONE).wait_send()

    def right_group(p, s, h):
        def one(i, carry):
            off = 0 if h == 0 else h * (1 - 2 * (i // 2))
            start = pl.multiple_of((zat(off) * 2 + i % 2) * wb, wb)
            ubuf[s] = ubuf[s] + jnp.dot(
                rbuf[:, pl.ds(start, wb)],
                vbuf[p, s, pl.ds(start, wb), :],
                precision=EXACT_PREC,
                preferred_element_type=jnp.float32,
            )
            return carry

        lax.fori_loop(0, 2 if h in (0, hops) else 4, one, 0)

    def clear_products():
        def trip(i):
            for s in PAIR:
                ubuf[s, block(i), :] = jnp.zeros((ROWS, wa), jnp.float32)

        fold(trip, 3 * wb // ROWS)

    def mix():
        def trip(i):
            tiles = [[ubuf[s, pl.ds(pl.multiple_of(r * wb + i * ROWS, ROWS), ROWS), :] for s in PAIR] for r in TRIPLE]
            for t in PAIR:
                for l in TRIPLE:
                    acc = None
                    for r in TRIPLE:
                        for s in PAIR:
                            term = w_ref[((l * 3 + r) * 2 + s) * 2 + t] * tiles[r][s]
                            acc = term if acc is None else acc + term
                    tbuf[t, block(i), l * wa : (l + 1) * wa] = acc

        fold(trip, wb // ROWS, 1)
        clear_products()

    def left_product(t, xx, cc):
        start = pl.multiple_of((xx * 2 + cc) * 2 * wa, 2 * wa)
        return jnp.dot(
            tbuf[t], lbuf[:, pl.ds(start, 2 * wa)], precision=EXACT_PREC, preferred_element_type=jnp.float32
        )

    def sib_copy(t, i):
        return remote(ps.at[i % 2], rd.at[t, i], rd_s.at[i % 2], rd_r.at[t, i], sibling)

    def lane(theirs):
        return pl.ds(pl.multiple_of((1 - yl if theirs else yl) * wa, wa), wa)

    def half_copy(p, t, d, theirs):
        at = pl.ds(0 if d > 0 else half, half)
        slot, side = 0 if d > 0 else 1, 0 if theirs else 1
        src = rd.at[t, 0, at, lane(theirs)]
        return remote(src, hx.at[p, t, slot, side], hx_s.at[t, slot, side], hx_r.at[p, t, slot, side], x_next[d])

    def full_copy(p, t, d, theirs):
        slot, side = 0 if d > 0 else 1, 0 if theirs else 1
        src = rd.at[t, 1 + slot, :, lane(theirs)]
        return remote(src, fx.at[p, t, slot, side], fx_s.at[t, slot, side], fx_r.at[p, t, slot, side], x_next[d])

    def cross_copy(p, t):
        return remote(rd.at[t, 3, :, lane(True)], yx.at[p, t], yx_s.at[t], yx_r.at[p, t], yl_partner)

    def left_stage(p, t, i):
        xx = (x + (2, 1, nx - 1, 0)[i]) % nx
        if i >= 2:
            sib_copy(t, i - 2).wait_send()
        elif t:
            sib_copy(0, i + 2).wait_send()
        ps[i % 2] = left_product(t, xx, 1 - c)
        sib_copy(t, i).start()
        po[...] = left_product(t, xx, c)
        sib_copy(t, i).wait_recv()
        for theirs in (GONE, HERE):
            lanes_at = lane(theirs)
            side = 0 if theirs else 1
            if i in (1, 2):
                half_copy(p, t, 1 if i == 1 else -1, theirs).wait_recv()
                base = 0 if i == 1 else half

                def add_half(k):
                    rows = pl.ds(pl.multiple_of(k * ROWS + base, ROWS), ROWS)
                    rd[t, i, rows, lanes_at] = rd[t, i, rows, lanes_at] + hx[p, t, i - 1, side, block(k), :]

                fold(add_half, half // ROWS)

            def add(k):
                rows = block(k)
                rd[t, i, rows, lanes_at] = rd[t, i, rows, lanes_at] + po[rows, lanes_at]

            fold(add, wb // ROWS)
            if i == 0:
                half_copy(p, t, 1, theirs).start()
                half_copy(p, t, -1, theirs).start()
            elif i < 3:
                full_copy(p, t, 1 if i == 1 else -1, theirs).start()

    def close_half(p, t):
        for theirs in (GONE, HERE):
            lanes_at = lane(theirs)
            side = 0 if theirs else 1
            for d in WAYS:
                full_copy(p, t, d, theirs).wait_recv()

            def add(k):
                rows = block(k)
                rd[t, 3, rows, lanes_at] = rd[t, 3, rows, lanes_at] + fx[p, t, 0, side, rows, :] + fx[p, t, 1, side, rows, :]

            fold(add, wb // ROWS)
            if theirs:
                cross_copy(p, t).start()
        cross_copy(p, t).wait_recv()
        alpha, beta, old = sc[0], sc[1], sc[2]
        mine = lane(False)

        def step(k):
            rows = block(k)
            g = rd[t, 3, rows, mine] + yx[p, t, rows, :]
            w_now, w_old = vbuf[p, t, own_block(k), :], vbuf[1 - p, t, own_block(k), :]
            vbuf[1 - p, t, own_block(k), :] = (g - alpha * w_now - old * w_old) / beta

        fold(step, wb // ROWS)

    def drain_sums(p, t):
        for theirs in (GONE, HERE):
            for d in WAYS:
                half_copy(p, t, d, theirs).wait_send()
                full_copy(p, t, d, theirs).wait_send()
        cross_copy(p, t).wait_send()

    def l_load(l):
        return pltpu.make_async_copy(
            l_hbm.at[l, pl.ds(pl.multiple_of(yl * wa, ROWS), wa), :], lbuf.at[pl.ds(l * wa, wa), :], ld_s.at[l]
        )

    def r_load(r):
        return pltpu.make_async_copy(
            r_hbm.at[r], rbuf.at[pl.ds(pl.multiple_of(r * wb + sub * half, ROWS), half), :], ld_s.at[3 + r]
        )

    def psi_at(s, of_sub):
        return vbuf.at[0, s, pl.ds(pl.multiple_of(own * wb + of_sub * half, ROWS), half), :]

    def psi_load(s):
        return pltpu.make_async_copy(psi_ref.at[yl, s], psi_at(s, sub), ld_s.at[6 + s])

    def psi_copy(s, gone):
        return remote(psi_ref.at[1 - yl, s], psi_at(s, sub if gone else 1 - sub), io_s.at[s], io_r.at[s], yl_partner)

    for s in PAIR:
        psi_load(s).start()
        psi_copy(s, GONE).start()
    for r in TRIPLE:
        r_copy(0, r, GONE).start()
        r_load(r).start()
    for l in TRIPLE:
        l_load(l).start()
    for t in PAIR:
        pl.semaphore_signal(credit.at[t], inc=1, device_id=sibling, device_id_type=MESH)

    def clear(i):
        for s in PAIR:
            vbuf[1, s, own_block(i), :] = jnp.zeros((ROWS, wa), jnp.float32)
            for p in PAIR:
                vv[p, s, block(i), :] = jnp.zeros((ROWS, wa), jnp.float32)

    fold(clear, wb // ROWS)
    clear_products()
    sc[2] = jnp.zeros((ROWS, wa), jnp.float32)
    for s in PAIR:
        psi_load(s).wait()
        psi_copy(s, HERE).wait_recv()
        own_sends(0, s)

    early = 1 + 3 * min(2, hops - 1) + (1 if hops > 2 else 0)
    for n, event in enumerate(events(0, 0)[:early]):
        event()
        if n in (3, 6):
            r_first((n - 3) // 3)
    for r in range(3 if early <= 3 else (2 if early <= 6 else 1)):
        r_first((2 if early > 6 else 1 if early > 3 else 0) + r)
    for r in TRIPLE:
        r_load(r).wait()
        l_load(r).wait()
    for s in PAIR:
        psi_copy(s, GONE).wait_send()

    def lanczos_step(j, carry):
        p = j % 2
        slot = (j + LANCZOS_STEPS - 1) % LANCZOS_STEPS
        more = j < LANCZOS_STEPS - 1
        late0 = events(p, 0)[early:]
        all1 = events(p, 1)

        all1.pop(0)()
        alpha_open(p)
        while late0:
            late0.pop(0)()
            if len(all1) > 3 * (hops - 1) and len(late0) % 2 == 0:
                all1.pop(0)()
        sum_send(0, 1, sum_take(0, 0))
        for h in range(hops + 1):
            take_cross(p, 0, h)

        @pl.when(j == 0)
        def _():
            for r in TRIPLE:
                r_second(r)
            r_last()

        marks = [
            ((0, 1), lambda: sum_send(0, 2, sum_take(0, 1))),
            ((0, hops), lambda: (alpha_close(sum_take(0, 2), slot), beta_open(p))),
            ((1, hops - 1), lambda: sum_send(1, 1, sum_take(1, 0))),
        ]
        for s in PAIR:
            for h in range(hops + 1):
                if s:
                    while len(all1) > 3 * (hops - h):
                        all1.pop(0)()
                    take_cross(p, 1, h)
                right_group(p, s, h)
                if all1:
                    all1.pop(0)()
                for where, mark in marks:
                    if where == (s, h):
                        mark()
        sum_send(1, 2, sum_take(1, 1))
        mix()
        for s in PAIR:
            drain_sends(p, s)

        ahead = events(1 - p, 0)[:early]

        def serve(count):
            @pl.when(more)
            def _():
                for _ in range(min(count, len(ahead))):
                    ahead.pop(0)()

        for t in PAIR:
            pl.semaphore_wait(credit.at[t], 1)
        for i in range(4):
            left_stage(p, 0, i)
            if i == 1:
                beta_close(p, sum_take(1, 2), slot)
        left_stage(p, 1, 0)
        close_half(p, 0)

        @pl.when(more)
        def _():
            own_sends(1 - p, 0)

        for i in range(1, 4):
            left_stage(p, 1, i)
            serve(2)
        serve(early)
        close_half(p, 1)

        @pl.when(more)
        def _():
            own_sends(1 - p, 1)

        for i in (2, 3):
            sib_copy(1, i).wait_send()
        for t in PAIR:
            drain_sums(p, t)

        @pl.when(more)
        def _():
            for t in PAIR:
                pl.semaphore_signal(credit.at[t], inc=1, device_id=sibling, device_id_type=MESH)

        sc[2] = jnp.where(j > 0, sc[1], jnp.zeros((ROWS, wa), jnp.float32))
        return carry

    lax.fori_loop(0, LANCZOS_STEPS, lanczos_step, 0)

    p = LANCZOS_STEPS % 2
    alpha_open(p)
    for stage in (1, 2):
        sum_send(0, stage, sum_take(0, stage - 1))
    alpha_close(sum_take(0, 2), LANCZOS_STEPS - 1)
    beta_open(p)
    for stage in (1, 2):
        sum_send(1, stage, sum_take(1, stage - 1))
    beta_close(p, sum_take(1, 2), LANCZOS_STEPS - 1)

    def out_store(s):
        src = vv.at[1 - p, s, pl.ds(pl.multiple_of(sub * half, ROWS), half), :]
        return pltpu.make_async_copy(src, vout_ref.at[yl, s], ld_s.at[6 + s])

    def out_copy(s, gone):
        src = vv.at[1 - p, s, pl.ds(pl.multiple_of((1 - sub) * half, ROWS), half), :]
        return remote(src, vout_ref.at[yl if gone else 1 - yl, s], io_s.at[2 + s], io_r.at[2 + s], yl_partner)

    for s in PAIR:
        out_copy(s, GONE).start()
        out_store(s).start()
    for s in PAIR:
        out_store(s).wait()
        out_copy(s, GONE).wait_send()
        out_copy(s, HERE).wait_recv()


def solution(mesh):
    nz, nx = mesh.shape["col"] // 4, mesh.shape["row"] // 2

    def local_steps(psi_blk, left_blk, mpo_tensor, right_blk):
        wa, wb = psi_blk.shape[0] // 2, psi_blk.shape[2] * 2
        da, db = left_blk.shape[2], right_blk.shape[2]
        half = wb // 2
        hops = nz // 2
        n0 = wb * 9 // 16 // 16 * 16
        lanes = 128 if wa % 128 == 0 else wa
        f32 = jnp.float32
        psi_t = jnp.transpose(psi_blk.reshape(2, wa, 2, half), (0, 2, 3, 1))
        kernel = functools.partial(lanczos_kernel, nz, nx, wa, wb, n0)
        vmem, dma = pltpu.VMEM, pltpu.SemaphoreType.DMA
        ids = 8 * hops + 2
        scalars, v_out = pl.pallas_call(
            kernel,
            out_shape=(
                jax.ShapeDtypeStruct((2 * LANCZOS_STEPS, ROWS, lanes), f32),
                jax.ShapeDtypeStruct((2, 2, half, wa), f32),
            ),
            in_specs=[
                pl.BlockSpec(memory_space=pl.ANY),
                pl.BlockSpec(memory_space=pl.ANY),
                pl.BlockSpec(memory_space=pltpu.SMEM),
                pl.BlockSpec(memory_space=pl.ANY),
            ],
            out_specs=(pl.BlockSpec(memory_space=pltpu.VMEM), pl.BlockSpec(memory_space=pl.ANY)),
            scratch_shapes=[
                vmem((2, 2, db, wa), f32),
                vmem((3 * wa, da), f32),
                vmem((3 * wb, db), f32),
                vmem((2, 3 * wb, wa), f32),
                vmem((2, wb, 3 * wa), f32),
                vmem((2, 2, wb, wa), f32),
                vmem((2, 4, wb, 2 * wa), f32),
                vmem((2, wb, 2 * wa), f32),
                vmem((wb, 2 * wa), f32),
                vmem((2, 2, 2, 2, half, wa), f32),
                vmem((2, 2, 2, 2, wb, wa), f32),
                vmem((2, 2, wb, wa), f32),
                vmem((2, nx * 2 + 4 + nz, ROWS, lanes), f32),
                vmem((3, ROWS, wa), f32),
                dma((2, ids)),
                dma((2, 2, ids)),
                dma((2,)),
                dma((2, 4)),
                dma((2, 2, 2)),
                dma((2, 2, 2, 2)),
                dma((2, 2, 2)),
                dma((2, 2, 2, 2)),
                dma((2,)),
                dma((2, 2)),
                dma((2, 3)),
                dma((2, 3)),
                dma((4, 3)),
                dma((4, 3)),
                dma((4,)),
                dma((4,)),
                dma((8,)),
                pltpu.SemaphoreType.REGULAR((2,)),
            ],
            compiler_params=pltpu.CompilerParams(has_side_effects=True, vmem_limit_bytes=66 * 1000 * 1000),
            name="lanczos",
        )(psi_t, jnp.transpose(left_blk, (1, 0, 2)), mpo_tensor.reshape(-1), jnp.transpose(right_blk, (1, 0, 2)))
        v_next = jnp.transpose(v_out, (0, 3, 1, 2)).reshape(psi_blk.shape)
        return scalars[:LANCZOS_STEPS, 0, 0], scalars[LANCZOS_STEPS:, 0, 0], v_next

    return jax.shard_map(
        local_steps,
        mesh=mesh,
        in_specs=(P("row", None, "col"), P("row", None, None), P(), P("col", None, None)),
        out_specs=(P(), P(), P("row", None, "col")),
        check_vma=False,
    )
```

time: 2490 us -> 520 us (0.21)
  waiting for transfers between devices: 1050 us -> 0 us
  blocking collectives: 1040 us -> 0 us
  Pallas kernels: 0 us -> 511 us
  matrix products: 246 us -> 0 us
  local copies, waits for them, and re-layouts: 91.8 us -> 7.25 us
  other arithmetic: 26.8 us -> 0 us
    psum x9 -> x0, blocking collectives: 1040 us -> none  [global_dot(): return lax.psum(jnp.sum(left_vec * right_vec), all_axes)]
    reduce_scatter x4 -> x0, waiting for transfers between devices: 959 us -> none  [apply_ham(): return lax.psum_scatter(y_part, 'col', scatter_dimension=2, tiled=True)]
    pallas_call x0 -> x1, Pallas kernels: none -> 511 us  [local_steps(): pl.pallas_call(kernel, out_shape=(jax.ShapeDtypeStruct((2 * LANCZOS_STEPS...]
    dot_general x12 -> x0, matrix products: 246 us -> none  [the longest x4 125 us: apply_ham(): jnp.einsum('cbrt,brd->ctd', t_two, right_blk, precision=EXACT_PREC, prefe...]
    all_gather x4 -> x0, waiting for transfers between devices: 92.9 us -> none  [apply_ham(): vec_rows = lax.all_gather(vec_blk, 'row', axis=0, tiled=True)]
    all_to_all x2 -> x0, local copies, waits for them, and re-layouts: 47.1 us -> none  [local_steps(): left_cols = lax.all_to_all(left_blk, 'row', 2, 0, tiled=True)]
    unnamed x10 -> x2, local copies, waits for them, and re-layouts: 36.3 us -> 2.01 us
  transfers between devices with their start and end apart: 9 -> 0, of which waited for: 7 -> 0; matrix products, arithmetic and copies ran while one was open for 2% -> 0% of each run, Pallas kernels for 0% -> 0%
where the time goes in v1:
time: 520 us; the launch traced here: 519 us
  Pallas kernels  511 us (98%)
  local copies, waits for them, and re-layouts  7.25 us (1%)
    pallas_call x1, Pallas kernels, local_steps(): pl.pallas_call(kernel, out_shape=(jax.ShapeDtypeStruct((2 * LANCZOS_STEPS...  511 us

profile of v1, /device:TPU:1, one launch (start us, length us, event | category | flops | bytes accessed | tf_op | source)
XLA Modules:
  0.0 518.7 jit_solution(14635667062121403876)
XLA Ops:
  0.6 0.8 copy.10
  1.4 0.6 reshape.16.w_ref
  2.0 2.0 copy.9
  4.1 510.8 %lanczos.1 = (f32[8,8,128]{2,1,0:T(8,128)}, f32[2,2,128,256]{3,2,1,0:T(8,128)}) custom-call(f32[2,2,128,256]{3,2,1,0:T(8,128)} %bitcast.8, f32[3,512,4096]{2,1,0:T(8,128)} %bitcast.6, f32[36]{0:T(128)} %reshape.16.w_ref, f32[3,128,4096]{2,1,0:T(8,128)} %bitcast.7), custom_call_target="tpu_custom_call" | custom-call | tf_op jit(solution)/shard_map/lanczos/pallas_call | solution.py:572
  514.9 1.4 slice_reduce_fusion
  516.2 1.2 copy.11
  517.5 1.2 copy.12

commit v2 on v0

v2 whole, which is shorter than its diff:
```python
import functools

import jax
import jax.numpy as jnp
from jax import lax
from jax.experimental import pallas as pl
from jax.experimental.pallas import tpu as pltpu
from jax.sharding import PartitionSpec as P

LANCZOS_STEPS = 4
EXACT_PREC = lax.Precision.HIGHEST
MESH = pl.DeviceIdType.MESH
ROWS = 8
SPLIT = 2
PIECES = 4
GATHER_ORDER = (
    "h201,a0,h211,h122,a1,p3,h103,h113,h221,m00*,h301,m01+,h311",
    "a2,m01-,h202,m02+,h212,h123,m02-,h321,h104,m03+,h114,h222",
    "m03-,h302,m10*,h312,m11+,h203,b0,h213,h124,m04*,h322,m11-",
    "h223,b1,m12+,h303,m12-,h313,h204,b2,h214,h323,h224,m13+,h304",
    "h314,h324,m13-,m14*",
)
REDUCE_ORDER = (
    "l00,f000,l01,l02,f030,f010,f020,d0,f011,f021,b3,l10,f100,l11",
    "o0,l12,f130,l20,c0,f110,f120,f111,f121,f200,l21,l22,h001,p0",
    "h011,f230,o1,l30,f300,h002,l31,h021,f210,c1,f220,l32,h012",
    "h003,f211,f221,f330,f310,f320,f311,f321,h022,p1,h101,o2,h111",
    "h013,h004,h023,c2,h121,o3,h102,h112,h014,p2,h024,c3",
)
PAIR = range(2)
TRIPLE = range(3)
WAYS = (1, -1)
GONE, HERE = True, False


def fold(body, count, unroll=4):
    while count % unroll:
        unroll //= 2

    def trip(i, carry):
        for u in range(unroll):
            body(i * unroll + u)
        return carry

    lax.fori_loop(0, count // unroll, trip, 0)


def lanczos_kernel(
    nz, nx, wa, wb,
    psi_ref, l_hbm, w_ref, r_hbm,
    scal_ref, vout_ref,
    vbuf, lbuf, rbuf, ubuf, tbuf, vv, rd, yb, hx, fx, yx, ob, red, sc,
    ag_s, ag_r, rd_s, rd_r, hx_s, hx_r, fx_s, fx_r, yx_s, yx_r,
    ar_s, ar_r, rr_s, rr_r, io_s, io_r, ld_s, credit,
):
    hops = nz // 2
    half, mb = wb // 2, wb // SPLIT
    quart = half // 4
    bit = quart // PIECES
    chunks = range(2 * SPLIT)
    col, row = lax.axis_index("col"), lax.axis_index("row")
    z, y, x, c = col // 4, col % 4, row // 2, row % 2
    yh, yl, sub = y // 2, ((y + 1) // 2) % 2, y % 2
    own = z * 2 + yh

    def dev(zz=None, yy=None, xx=None, cc=None):
        zz = z if zz is None else zz
        yy = y if yy is None else yy
        xx = x if xx is None else xx
        cc = c if cc is None else cc
        return {"col": zz * 4 + yy, "row": xx * 2 + cc}

    def zat(off):
        return (z + off + 2 * nz) % nz

    sibling = dev(cc=1 - c)
    yl_partner = dev(yy=y + 1 - 2 * sub)
    yh_partner = dev(yy=3 - y)
    x_mate = dev(xx=x + 1 - 2 * (x % 2))
    z_next = {1: dev(zz=zat(1)), -1: dev(zz=zat(-1))}
    x_next = {1: dev(xx=(x + 1) % nx), -1: dev(xx=(x + nx - 1) % nx)}

    def remote(src, dst, send, recv, to):
        return pltpu.make_async_remote_copy(
            src_ref=src, dst_ref=dst, send_sem=send, recv_sem=recv, device_id=to, device_id_type=MESH
        )

    def span(start, count):
        return pl.ds(pl.multiple_of(start, ROWS), count)

    def block(i):
        return span(i * ROWS, ROWS)

    def piece(p, q, k, kind, d, h, mid, to):
        cut = mb // 2 + (q % SPLIT) * mb // 8
        start, count = (0, cut) if kind == 0 else (cut, mb - cut)
        if h == hops:
            count //= 2
            start += count if d < 0 else 0
        at = vbuf.at[p, q // SPLIT, span(k * wb + (q % SPLIT) * mb + start, count), :]
        return remote(at, at, ag_s.at[q, mid], ag_r.at[p, q, mid], to)

    def z_copy(p, q, d, line, h, gone):
        k = zat(-d * (h - 1 if gone else h)) * 2 + (1 - yh if line == 2 else yh)
        mid = ((0 if d > 0 else 3) + line) * hops + h - 1
        return piece(p, q, k, min(line, 1), d, h, mid, z_next[d])

    def pair_copy(p, q, kind, d, h, gone):
        mid = 6 * hops + (2 * h + max(d, 0) if h else 0 if kind else 1)
        return piece(p, q, zat(-d * h) * 2 + (yh if gone else 1 - yh), kind, d, h, mid, yh_partner)

    def own_sends(p, q):
        pair_copy(p, q, 1, 0, 0, GONE).start()
        for line in PAIR:
            for d in WAYS:
                z_copy(p, q, d, line, 1, GONE).start()
        pair_copy(p, q, 0, 0, 0, GONE).start()

    def take_pair(p, q):
        pair_copy(p, q, 1, 0, 0, HERE).wait_recv()
        for d in WAYS:
            z_copy(p, q, d, 2, 1, GONE).start()

    def take_hop(p, q, line, h):
        for d in WAYS:
            z_copy(p, q, d, line, h, HERE).wait_recv()
            if h < hops:
                z_copy(p, q, d, line, h + 1, GONE).start()
            if line == 0:
                pair_copy(p, q, 0, d, h, GONE).start()

    def drain_gather(p):
        for q in chunks:
            for kind in PAIR:
                pair_copy(p, q, kind, 0, 0, GONE).wait_send()
            for d in WAYS:
                for h in range(1, hops + 1):
                    for line in TRIPLE:
                        z_copy(p, q, d, line, h, GONE).wait_send()
                    pair_copy(p, q, 0, d, h, GONE).wait_send()

    groups = (
        (0, nx * 2, row, lambda d: {"col": col, "row": (row + d) % (nx * 2)}),
        (nx * 2, 4, y, lambda d: dev(yy=(y + d) % 4)),
        (nx * 2 + 4, nz, z, lambda d: dev(zz=(z + d) % nz)),
    )

    def sum_send(which, stage, tile):
        base, count, me, peer = groups[stage]
        red[which, base + me] = tile
        at = red.at[which, base + me]
        for d in range(1, count):
            remote(at, at, ar_s.at[which, stage], ar_r.at[which, stage], peer(d)).start()

    def sum_take(which, stage):
        base, count, _, _ = groups[stage]
        at = red.at[which, pl.ds(base, count - 1)]
        pltpu.make_async_copy(at, at, ar_r.at[which, stage]).wait()
        pltpu.make_async_copy(at, at, ar_s.at[which, stage]).wait()
        total = red[which, base]
        for i in range(1, count):
            total = total + red[which, base + i]
        return total

    def sum_pass(which, stage):
        sum_send(which, stage, sum_take(which, stage - 1))

    lanes = red.shape[-1]

    def narrow(tile):
        out = tile[:, :lanes]
        for i in range(1, wa // lanes):
            out = out + tile[:, i * lanes : (i + 1) * lanes]
        return out

    def own_block(i):
        return span(own * wb + i * ROWS, ROWS)

    def accumulate(term):
        def trip(i, acc):
            for s in PAIR:
                acc = acc + term(s, i)
            return acc

        return lax.fori_loop(0, wb // ROWS, trip, jnp.zeros((ROWS, wa), jnp.float32), unroll=4)

    def alpha_open(p):
        acc = accumulate(lambda s, i: vv[p, s, block(i), :] * vbuf[p, s, own_block(i), :])
        sum_send(0, 0, narrow(acc))

    def alpha_close(slot):
        value = jnp.full((ROWS, wa), jnp.sum(sum_take(0, 2)), jnp.float32)
        sc[0] = value
        scal_ref[slot] = value[:, :lanes]

    def beta_open(p):
        alpha, beta = sc[0], sc[2]

        def term(s, i):
            u = vbuf[p, s, own_block(i), :] - alpha * vv[p, s, block(i), :] - beta * vv[1 - p, s, block(i), :]
            vv[1 - p, s, block(i), :] = u
            return u * u

        sum_send(1, 0, narrow(accumulate(term)))

    def beta_close(slot):
        value = jnp.sqrt(jnp.full((ROWS, wa), jnp.sum(sum_take(1, 2)), jnp.float32))
        sc[1] = value
        scal_ref[LANCZOS_STEPS + slot] = value[:, :lanes]

    def scale(p):
        def trip(i):
            for s in PAIR:
                vv[1 - p, s, block(i), :] = vv[1 - p, s, block(i), :] / sc[1]

        fold(trip, wb // ROWS)

    def r_rows(e, of_sub, q):
        return rbuf.at[span((e // PIECES) * wb + of_sub * half + q * quart + (e % PIECES) * bit, bit), :]

    q_own, q_mate = (x % 2) * 2 + c, (1 - x % 2) * 2 + c
    q_sib, q_sib_mate = (x % 2) * 2 + 1 - c, (1 - x % 2) * 2 + 1 - c

    def r_copy(way, e, gone):
        sems = rr_s.at[way, e], rr_r.at[way, e]
        if way == 0:
            src = r_hbm.at[e // PIECES, span(q_own * quart + (e % PIECES) * bit, bit), :]
            return remote(src, r_rows(e, sub if gone else 1 - sub, q_own), *sems, yl_partner)
        here, there = (q_mate, q_sib_mate) if way == 3 else (q_own, q_mate if way == 1 else q_sib)
        at = r_rows(e, 1 - sub, here if gone else there)
        return remote(at, at, *sems, x_mate if way == 1 else sibling)

    def r_first(e):
        r_copy(0, e, HERE).wait_recv()
        r_copy(1, e, GONE).start()
        r_copy(2, e, GONE).start()

    def r_second(e):
        r_copy(1, e, HERE).wait_recv()
        r_copy(3, e, GONE).start()

    def r_last():
        for e in range(3 * PIECES):
            r_copy(2, e, HERE).wait_recv()
            r_copy(3, e, HERE).wait_recv()
            for way in range(4):
                r_copy(way, e, GONE).wait_send()

    def right_group(p, s, h, way):
        d = 1 if way == "+" else -1
        for q in range(s * SPLIT, s * SPLIT + SPLIT):
            for e in (d,) if way != "*" else WAYS if h else (0,):
                pair_copy(p, q, 0, e, h, HERE).wait_recv()

        def one(i, carry):
            start = pl.multiple_of((zat(-d * h) * 2 + i) * wb, wb)
            ubuf[s] = ubuf[s] + jnp.dot(
                rbuf[:, pl.ds(start, wb)],
                vbuf[p, s, pl.ds(start, wb), :],
                precision=EXACT_PREC,
                preferred_element_type=jnp.float32,
            )
            return carry

        lax.fori_loop(0, 2, one, 0)

    def clear_products():
        def trip(i):
            for s in PAIR:
                ubuf[s, block(i), :] = jnp.zeros((ROWS, wa), jnp.float32)

        fold(trip, 3 * wb // ROWS)

    def mix():
        def trip(i):
            tiles = [[ubuf[s, span(r * wb + i * ROWS, ROWS), :] for s in PAIR] for r in TRIPLE]
            for t in PAIR:
                for l in TRIPLE:
                    acc = None
                    for r in TRIPLE:
                        for s in PAIR:
                            term = w_ref[((l * 3 + r) * 2 + s) * 2 + t] * tiles[r][s]
                            acc = term if acc is None else acc + term
                    tbuf[t, block(i), l * wa : (l + 1) * wa] = acc

        fold(trip, wb // ROWS, 1)
        clear_products()

    def sib_copy(q, i):
        return remote(yb.at[i], rd.at[q, i], rd_s.at[i], rd_r.at[q, i], sibling)

    def left_products(q, part):
        def one(n, carry):
            theirs = n < (2, 2, 0)[part]
            i = n % 2 if part == 0 else n + 3 - part
            away = jnp.where(i < 2, i + 2, 3 - i)
            start = (((x + away) % nx) * 2 + jnp.where(theirs, 1 - c, c)) * 2 * wa
            yb[jnp.where(theirs, i, i + 4)] = jnp.dot(
                tbuf[q // SPLIT, (q % SPLIT) * mb : (q % SPLIT + 1) * mb, :],
                lbuf[:, pl.ds(pl.multiple_of(start, 2 * wa), 2 * wa)],
                precision=EXACT_PREC,
                preferred_element_type=jnp.float32,
            )

            @pl.when(theirs)
            def _():
                sib_copy(q, i).start()

            return carry

        for i in ((0, 1), (2, 3), ())[part] if q else ():
            sib_copy(q - 1, i).wait_send()
        lax.fori_loop(0, (3, 2, 3)[part], one, 0)

    def lane(theirs):
        return pl.ds(pl.multiple_of((1 - yl if theirs else yl) * wa, wa), wa)

    def half_copy(p, q, d, theirs):
        slot, side = 0 if d > 0 else 1, 0 if theirs else 1
        src = rd.at[q, 0, pl.ds(slot * mb // 2, mb // 2), lane(theirs)]
        return remote(src, hx.at[p, q, slot, side], hx_s.at[q, slot, side], hx_r.at[p, q, slot, side], x_next[d])

    def full_copy(p, q, d, theirs):
        slot, side = 0 if d > 0 else 1, 0 if theirs else 1
        src = rd.at[q, 2 - slot, :, lane(theirs)]
        return remote(src, fx.at[p, q, slot, side], fx_s.at[q, slot, side], fx_r.at[p, q, slot, side], x_next[d])

    def cross_copy(p, q):
        return remote(rd.at[q, 3, :, lane(GONE)], yx.at[p, q], yx_s.at[q], yx_r.at[p, q], yl_partner)

    def left_sum(p, q, i, side):
        if side == 0:
            sib_copy(q, i).wait_recv()

            def add(k):
                rows = block(k)
                rd[q, i, rows, :] = rd[q, i, rows, :] + yb[i + 4, rows, :]

            fold(add, mb // ROWS)
        if i == 0:
            for theirs in (GONE, HERE):
                for d in WAYS:
                    half_copy(p, q, d, theirs).start()
        elif i < 3:
            d, theirs = 2 * i - 3, side == 0
            lanes_at = lane(theirs)
            half_copy(p, q, d, theirs).wait_recv()

            def add_half(k):
                rows = span(k * ROWS + (0 if d > 0 else mb // 2), ROWS)
                rd[q, i, rows, lanes_at] = rd[q, i, rows, lanes_at] + hx[p, q, i % 2, side, block(k), :]

            fold(add_half, mb // 2 // ROWS)
            full_copy(p, q, d, theirs).start()

    def chip_sum(p, q, theirs):
        lanes_at, side = lane(theirs), 0 if theirs else 1
        for d in WAYS:
            full_copy(p, q, d, theirs).wait_recv()

        def add(k):
            rows = block(k)
            rd[q, 3, rows, lanes_at] = rd[q, 3, rows, lanes_at] + fx[p, q, 0, side, rows, :] + fx[p, q, 1, side, rows, :]

        fold(add, mb // ROWS)

    def open_cross(p, q):
        chip_sum(p, q, GONE)
        cross_copy(p, q).start()

    def close_chunk(p, q, more):
        chip_sum(p, q, HERE)
        cross_copy(p, q).wait_recv()
        alpha, beta, old = sc[0], sc[1], sc[2]
        s, mine = q // SPLIT, lane(HERE)

        def step(k):
            rows, at = block(k), own_block(k + (q % SPLIT) * mb // ROWS)
            g = rd[q, 3, rows, mine] + yx[p, q, rows, :]
            vbuf[1 - p, s, at, :] = (g - alpha * vbuf[p, s, at, :] - old * vbuf[1 - p, s, at, :]) / beta

        fold(step, mb // ROWS)

        @pl.when(more)
        def _():
            own_sends(1 - p, q)

    def drain_sums(p, q):
        for theirs in (GONE, HERE):
            for d in WAYS:
                half_copy(p, q, d, theirs).wait_send()
                full_copy(p, q, d, theirs).wait_send()
        cross_copy(p, q).wait_send()

    def l_load(l):
        return pltpu.make_async_copy(l_hbm.at[l, span(yl * wa, wa), :], lbuf.at[pl.ds(l * wa, wa), :], ld_s.at[l])

    def r_load(r):
        return pltpu.make_async_copy(r_hbm.at[r], rbuf.at[span(r * wb + sub * half, half), :], ld_s.at[3 + r])

    def psi_at(s, of_sub):
        return vbuf.at[0, s, span(own * wb + of_sub * half, half), :]

    def psi_load(s):
        return pltpu.make_async_copy(psi_ref.at[yl, s], psi_at(s, sub), ld_s.at[6 + s])

    def psi_copy(s, gone):
        return remote(psi_ref.at[1 - yl, s], psi_at(s, sub if gone else 1 - sub), io_s.at[s], io_r.at[s], yl_partner)

    for s in PAIR:
        psi_load(s).start()
        psi_copy(s, GONE).start()
    for e in range(3 * PIECES):
        r_copy(0, e, GONE).start()
    for r in TRIPLE:
        r_load(r).start()
    for l in TRIPLE:
        l_load(l).start()
    pl.semaphore_signal(credit, inc=1, device_id=sibling, device_id_type=MESH)

    def clear(i):
        for s in PAIR:
            vbuf[1, s, own_block(i), :] = jnp.zeros((ROWS, wa), jnp.float32)
            for p in PAIR:
                vv[p, s, block(i), :] = jnp.zeros((ROWS, wa), jnp.float32)

    fold(clear, wb // ROWS)
    clear_products()
    sc[2] = jnp.zeros((ROWS, wa), jnp.float32)
    def work(name, p, more, slot):
        kind, tail = name[0], name[1:]
        if kind == "m":
            return functools.partial(right_group, p, int(tail[0]), int(tail[1]), tail[2])
        args = [int(digit) for digit in tail]
        if kind in "ab":
            calls = {
                "a0": lambda: alpha_open(p),
                "b0": lambda: (alpha_close(slot), beta_open(p)),
                "b3": lambda: (beta_close(slot), scale(p)),
            }
            return calls.get(name, functools.partial(sum_pass, "ab".index(kind), args[0]))
        if kind == "c":
            return functools.partial(close_chunk, p, *args, more)
        if kind == "d":
            return functools.partial(drain_gather, p)
        if kind == "l":
            return functools.partial(left_products, *args)
        return functools.partial({"p": take_pair, "h": take_hop, "f": left_sum, "o": open_cross}[kind], p, *args)

    gather_order = ",".join(GATHER_ORDER).split(",")
    reduce_order = ",".join(REDUCE_ORDER).split(",")
    r_plan = []
    for e in range(3 * PIECES + 2):
        if e < 3 * PIECES:
            r_plan.append(functools.partial(r_first, e))
        if e > 1:
            r_plan.append(functools.partial(r_second, e - 2))

    for s in PAIR:
        psi_load(s).wait()
        psi_copy(s, HERE).wait_recv()
        own_sends(0, s * SPLIT)
    served = [name for name in reduce_order if name[0] in "phc"]
    for n, name in enumerate(served):
        if name[0] != "c":
            work(name, 0, None, None)()
        elif int(name[1]) % SPLIT:
            own_sends(0, int(name[1]))
        if n % 3 > 0 and n * 3 > len(served):
            r_plan.pop(0)()
    for r in TRIPLE:
        r_load(r).wait()
        l_load(r).wait()
    for s in PAIR:
        psi_copy(s, GONE).wait_send()

    def lanczos_step(j, carry):
        p = j % 2
        slot = (j + LANCZOS_STEPS - 1) % LANCZOS_STEPS
        more = j < LANCZOS_STEPS - 1

        rest = list(r_plan)
        for name in gather_order:
            if name[0] == "m" and rest is not None or name[0] in "ph" and rest:
                now = len(rest) if name[0] == "m" else 2

                @pl.when(j == 0)
                def _():
                    for _ in range(min(now, len(rest))):
                        rest.pop(0)()
                    if name[0] == "m":
                        r_last()

                rest = None if name[0] == "m" else rest
            work(name, p, more, slot)()
        mix()

        pl.semaphore_wait(credit, 1)
        for name in reduce_order:
            if name[0] in "ph":
                pl.when(more)(work(name, 1 - p, more, slot))
            else:
                work(name, p, more, slot)()
        for i in range(4):
            sib_copy(chunks[-1], i).wait_send()
        for q in chunks:
            drain_sums(p, q)

        @pl.when(more)
        def _():
            pl.semaphore_signal(credit, inc=1, device_id=sibling, device_id_type=MESH)

        sc[2] = jnp.where(j > 0, sc[1], jnp.zeros((ROWS, wa), jnp.float32))
        return carry

    lax.fori_loop(0, LANCZOS_STEPS, lanczos_step, 0)

    p = LANCZOS_STEPS % 2

    def out_copy(s):
        src = vv.at[1 - p, s, span((1 - sub) * half, half), :]
        return remote(src, ob.at[s], io_s.at[2 + s], io_r.at[2 + s], yl_partner)

    alpha_open(p)
    sum_pass(0, 1)
    sum_pass(0, 2)
    alpha_close(LANCZOS_STEPS - 1)
    beta_open(p)
    for s in PAIR:
        out_copy(s).start()
    sum_pass(1, 1)
    sum_pass(1, 2)
    beta_close(LANCZOS_STEPS - 1)
    for s in PAIR:
        out_copy(s).wait_recv()

        def put(i):
            vout_ref[yl, s, block(i), :] = vv[1 - p, s, span(sub * half + i * ROWS, ROWS), :] / sc[1]
            vout_ref[1 - yl, s, block(i), :] = ob[s, block(i), :] / sc[1]

        fold(put, half // ROWS)
        out_copy(s).wait_send()


def solution(mesh):
    nz, nx = mesh.shape["col"] // 4, mesh.shape["row"] // 2

    def local_steps(psi_blk, left_blk, mpo_tensor, right_blk):
        wa, wb = psi_blk.shape[0] // 2, psi_blk.shape[2] * 2
        da, db = left_blk.shape[2], right_blk.shape[2]
        half = wb // 2
        hops = nz // 2
        mb = wb // SPLIT
        parts = 2 * SPLIT
        lanes = 128 if wa % 128 == 0 else wa
        f32 = jnp.float32
        psi_t = jnp.transpose(psi_blk.reshape(2, wa, 2, half), (0, 2, 3, 1))
        kernel = functools.partial(lanczos_kernel, nz, nx, wa, wb)
        vmem, dma = pltpu.VMEM, pltpu.SemaphoreType.DMA
        ids = 8 * hops + 2
        scalars, v_out = pl.pallas_call(
            kernel,
            out_shape=(
                jax.ShapeDtypeStruct((2 * LANCZOS_STEPS, ROWS, lanes), f32),
                jax.ShapeDtypeStruct((2, 2, half, wa), f32),
            ),
            in_specs=[
                pl.BlockSpec(memory_space=pl.ANY),
                pl.BlockSpec(memory_space=pl.ANY),
                pl.BlockSpec(memory_space=pltpu.SMEM),
                pl.BlockSpec(memory_space=pl.ANY),
            ],
            out_specs=(pl.BlockSpec(memory_space=pltpu.VMEM),) * 2,
            scratch_shapes=[
                vmem((2, 2, db, wa), f32),
                vmem((3 * wa, da), f32),
                vmem((3 * wb, db), f32),
                vmem((2, 3 * wb, wa), f32),
                vmem((2, wb, 3 * wa), f32),
                vmem((2, 2, wb, wa), f32),
                vmem((parts, 4, mb, 2 * wa), f32),
                vmem((8, mb, 2 * wa), f32),
                vmem((2, parts, 2, 2, mb // 2, wa), f32),
                vmem((2, parts, 2, 2, mb, wa), f32),
                vmem((2, parts, mb, wa), f32),
                vmem((2, half, wa), f32),
                vmem((2, nx * 2 + 4 + nz, ROWS, lanes), f32),
                vmem((3, ROWS, wa), f32),
                dma((parts, ids)),
                dma((2, parts, ids)),
                dma((4,)),
                dma((parts, 4)),
                dma((parts, 2, 2)),
                dma((2, parts, 2, 2)),
                dma((parts, 2, 2)),
                dma((2, parts, 2, 2)),
                dma((parts,)),
                dma((2, parts)),
                dma((2, 3)),
                dma((2, 3)),
                dma((4, 3 * PIECES)),
                dma((4, 3 * PIECES)),
                dma((4,)),
                dma((4,)),
                dma((8,)),
                pltpu.SemaphoreType.REGULAR,
            ],
            compiler_params=pltpu.CompilerParams(has_side_effects=True, vmem_limit_bytes=66 * 1000 * 1000),
            name="lanczos",
        )(psi_t, jnp.transpose(left_blk, (1, 0, 2)), mpo_tensor.reshape(-1), jnp.transpose(right_blk, (1, 0, 2)))
        v_next = jnp.transpose(v_out, (0, 3, 1, 2)).reshape(psi_blk.shape)
        return scalars[:LANCZOS_STEPS, 0, 0], scalars[LANCZOS_STEPS:, 0, 0], v_next

    return jax.shard_map(
        local_steps,
        mesh=mesh,
        in_specs=(P("row", None, "col"), P("row", None, None), P(), P("col", None, None)),
        out_specs=(P(), P(), P("row", None, "col")),
        check_vma=False,
    )
```

time: 2490 us -> 463 us (0.19)
  waiting for transfers between devices: 1050 us -> 0 us
  blocking collectives: 1040 us -> 0 us
  Pallas kernels: 0 us -> 455 us
  matrix products: 246 us -> 0 us
  local copies, waits for them, and re-layouts: 91.8 us -> 7.25 us
  other arithmetic: 26.8 us -> 0 us
    psum x9 -> x0, blocking collectives: 1040 us -> none  [global_dot(): return lax.psum(jnp.sum(left_vec * right_vec), all_axes)]
    reduce_scatter x4 -> x0, waiting for transfers between devices: 959 us -> none  [apply_ham(): return lax.psum_scatter(y_part, 'col', scatter_dimension=2, tiled=True)]
    pallas_call x0 -> x1, Pallas kernels: none -> 455 us  [local_steps(): pl.pallas_call(kernel, out_shape=(jax.ShapeDtypeStruct((2 * LANCZOS_STEPS...]
    dot_general x12 -> x0, matrix products: 246 us -> none  [the longest x4 125 us: apply_ham(): jnp.einsum('cbrt,brd->ctd', t_two, right_blk, precision=EXACT_PREC, prefe...]
    all_gather x4 -> x0, waiting for transfers between devices: 92.9 us -> none  [apply_ham(): vec_rows = lax.all_gather(vec_blk, 'row', axis=0, tiled=True)]
    all_to_all x2 -> x0, local copies, waits for them, and re-layouts: 47.1 us -> none  [local_steps(): left_cols = lax.all_to_all(left_blk, 'row', 2, 0, tiled=True)]
    unnamed x10 -> x2, local copies, waits for them, and re-layouts: 36.3 us -> 2.01 us
  transfers between devices with their start and end apart: 9 -> 0, of which waited for: 7 -> 0; matrix products, arithmetic and copies ran while one was open for 2% -> 0% of each run, Pallas kernels for 0% -> 0%
where the time goes in v2:
time: 463 us
  Pallas kernels  455 us (98%)
  local copies, waits for them, and re-layouts  7.25 us (2%)
    pallas_call x1, Pallas kernels, local_steps(): pl.pallas_call(kernel, out_shape=(jax.ShapeDtypeStruct((2 * LANCZOS_STEPS...  455 us

profile of v2, /device:TPU:1, one launch (start us, length us, event | category | flops | bytes accessed | tf_op | source)
XLA Modules:
  0.0 462.9 jit_solution(3021479162520349104)
XLA Ops:
  0.6 0.8 copy.10
  1.4 0.6 reshape.16.w_ref
  2.0 2.0 copy.9
  4.1 455.0 %lanczos.1 = (f32[8,8,128]{2,1,0:T(8,128)}, f32[2,2,128,256]{3,2,1,0:T(8,128)}) custom-call(f32[2,2,128,256]{3,2,1,0:T(8,128)} %bitcast.8, f32[3,512,4096]{2,1,0:T(8,128)} %bitcast.6, f32[36]{0:T(128)} %reshape.16.w_ref, f32[3,128,4096]{2,1,0:T(8,128)} %bitcast.7), custom_call_target="tpu_custom_call" | custom-call | tf_op jit(solution)/shard_map/lanczos/pallas_call | solution.py:561
  459.1 1.4 slice_reduce_fusion
  460.5 1.2 copy.11
  461.7 1.2 copy.12

commit v3 on v2

--- a/solution.py
+++ b/solution.py
@@ -12,20 +12,20 @@
 MESH = pl.DeviceIdType.MESH
 ROWS = 8
 SPLIT = 2
-PIECES = 4
+PIECES = 2
 GATHER_ORDER = (
-    "h201,a0,h211,h122,a1,p3,h103,h113,h221,m00*,h301,m01+,h311",
-    "a2,m01-,h202,m02+,h212,h123,m02-,h321,h104,m03+,h114,h222",
-    "m03-,h302,m10*,h312,m11+,h203,b0,h213,h124,m04*,h322,m11-",
-    "h223,b1,m12+,h303,m12-,h313,h204,b2,h214,h323,h224,m13+,h304",
-    "h314,h324,m13-,m14*",
+    "a0,h103,p2,h113,h123,h202,h212,h301,h311,m00*,h104,h221,m01+",
+    "h114,h124,m01-,h203,p3,h213,m02+,h302,m02-,h312,a1,m03+,h222",
+    "h204,m03-,h321,m10*,h214,h303,m11+,h313,m11-,h223,m04*,h322",
+    "b0,h304,m12+,h314,h224,m12-,h323,m13+,m13-,h324,b1,m14*",
 )
 REDUCE_ORDER = (
-    "l00,f000,l01,l02,f030,f010,f020,d0,f011,f021,b3,l10,f100,l11",
-    "o0,l12,f130,l20,c0,f110,f120,f111,f121,f200,l21,l22,h001,p0",
-    "h011,f230,o1,l30,f300,h002,l31,h021,f210,c1,f220,l32,h012",
-    "h003,f211,f221,f330,f310,f320,f311,f321,h022,p1,h101,o2,h111",
-    "h013,h004,h023,c2,h121,o3,h102,h112,h014,p2,h024,c3",
+    "l00,f000,l01,l02,f030,f010,f020,x1,d0,b3,f011,f021,l10,f100",
+    "l11,l12,f130,x2,l20,c0,f110,f120,f111,f121,f200,l21,l22,p0",
+    "h001,h011,f230,x3,l30,h021,c1,f300,l31,h002,h012,f210,f220",
+    "f211,f221,h022,l32,p1,h101,h111,f330,f310,f320,f311,f321",
+    "h003,h013,h023,h121,c2,h102,h112,h004,h014,h024,h122,h201",
+    "h211,c3",
 )
 PAIR = range(2)
 TRIPLE = range(3)
@@ -55,13 +55,14 @@
 ):
     hops = nz // 2
     half, mb = wb // 2, wb // SPLIT
-    quart = half // 4
-    bit = quart // PIECES
+    part = half // (2 * nx)
+    bit = part // PIECES
     chunks = range(2 * SPLIT)
     col, row = lax.axis_index("col"), lax.axis_index("row")
-    z, y, x, c = col // 4, col % 4, row // 2, row % 2
-    yh, yl, sub = y // 2, ((y + 1) // 2) % 2, y % 2
-    own = z * 2 + yh
+    div, mod = lax.div, lax.rem
+    z, y, x, c = div(col, 4), mod(col, 4), div(row, 2), mod(row, 2)
+    yh, sub = div(y, 2), mod(y, 2)
+    yl = mod(div(y + 1, 2), 2)
 
     def dev(zz=None, yy=None, xx=None, cc=None):
         zz = z if zz is None else zz
@@ -70,15 +71,18 @@
         cc = c if cc is None else cc
         return {"col": zz * 4 + yy, "row": xx * 2 + cc}
 
-    def zat(off):
-        return (z + off + 2 * nz) % nz
+    zs = {off: mod(z + off + nz, nz) for off in range(-hops, nz)}
+    xs = {off: mod(x + off + nx, nx) for off in range(-1, nx)}
+    starts = {off: (at * 2 + yh) * wb for off, at in zs.items()}
+    others = {off: (at * 2 + 1 - yh) * wb for off, at in zs.items()}
+    own = starts[0]
 
     sibling = dev(cc=1 - c)
     yl_partner = dev(yy=y + 1 - 2 * sub)
     yh_partner = dev(yy=3 - y)
-    x_mate = dev(xx=x + 1 - 2 * (x % 2))
-    z_next = {1: dev(zz=zat(1)), -1: dev(zz=zat(-1))}
-    x_next = {1: dev(xx=(x + 1) % nx), -1: dev(xx=(x + nx - 1) % nx)}
+    z_next = {d: dev(zz=zs[d]) for d in WAYS}
+    x_next = {d: dev(xx=xs[d]) for d in WAYS}
+    x_side = {d: dev(yy=y + 1 - 2 * sub, xx=xs[d]) for d in WAYS}
 
     def remote(src, dst, send, recv, to):
         return pltpu.make_async_remote_copy(
@@ -91,30 +95,36 @@
     def block(i):
         return span(i * ROWS, ROWS)
 
-    def piece(p, q, k, kind, d, h, mid, to):
-        cut = mb // 2 + (q % SPLIT) * mb // 8
-        start, count = (0, cut) if kind == 0 else (cut, mb - cut)
+    def cut(q):
+        return mb * (96, 96, 64, 32)[q] // 128
+
+    def lines(q):
+        return TRIPLE if cut(q) else TRIPLE[1:]
+
+    def piece(p, q, base, kind, d, h, mid, to):
+        start, count = (0, cut(q)) if kind == 0 else (cut(q), mb - cut(q))
         if h == hops:
             count //= 2
             start += count if d < 0 else 0
-        at = vbuf.at[p, q // SPLIT, span(k * wb + (q % SPLIT) * mb + start, count), :]
+        at = vbuf.at[p, q // SPLIT, span(base + (q % SPLIT) * mb + start, count), :]
         return remote(at, at, ag_s.at[q, mid], ag_r.at[p, q, mid], to)
 
     def z_copy(p, q, d, line, h, gone):
-        k = zat(-d * (h - 1 if gone else h)) * 2 + (1 - yh if line == 2 else yh)
+        base = (others if line == 2 else starts)[-d * (h - 1 if gone else h)]
         mid = ((0 if d > 0 else 3) + line) * hops + h - 1
-        return piece(p, q, k, min(line, 1), d, h, mid, z_next[d])
+        return piece(p, q, base, min(line, 1), d, h, mid, z_next[d])
 
     def pair_copy(p, q, kind, d, h, gone):
         mid = 6 * hops + (2 * h + max(d, 0) if h else 0 if kind else 1)
-        return piece(p, q, zat(-d * h) * 2 + (yh if gone else 1 - yh), kind, d, h, mid, yh_partner)
+        return piece(p, q, (starts if gone else others)[-d * h], kind, d, h, mid, yh_partner)
 
     def own_sends(p, q):
         pair_copy(p, q, 1, 0, 0, GONE).start()
-        for line in PAIR:
+        for line in lines(q)[:-1]:
             for d in WAYS:
                 z_copy(p, q, d, line, 1, GONE).start()
-        pair_copy(p, q, 0, 0, 0, GONE).start()
+        if cut(q):
+            pair_copy(p, q, 0, 0, 0, GONE).start()
 
     def take_pair(p, q):
         pair_copy(p, q, 1, 0, 0, HERE).wait_recv()
@@ -131,26 +141,30 @@
 
     def drain_gather(p):
         for q in chunks:
-            for kind in PAIR:
+            first = range(0 if cut(q) else 1, 2)
+            for kind in first:
                 pair_copy(p, q, kind, 0, 0, GONE).wait_send()
             for d in WAYS:
                 for h in range(1, hops + 1):
-                    for line in TRIPLE:
+                    for line in lines(q):
                         z_copy(p, q, d, line, h, GONE).wait_send()
-                    pair_copy(p, q, 0, d, h, GONE).wait_send()
-
+                    for _ in first[1:]:
+                        pair_copy(p, q, 0, d, h, GONE).wait_send()
+
+    plane = nx * 8
+
+    line = [mod(row * 4 + y + d, plane) for d in range(plane)]
     groups = (
-        (0, nx * 2, row, lambda d: {"col": col, "row": (row + d) % (nx * 2)}),
-        (nx * 2, 4, y, lambda d: dev(yy=(y + d) % 4)),
-        (nx * 2 + 4, nz, z, lambda d: dev(zz=(z + d) % nz)),
+        (0, plane, row * 4 + y, [{"col": z * 4 + mod(at, 4), "row": div(at, 4)} for at in line]),
+        (plane, nz, z, [dev(zz=zs[d]) for d in range(nz)]),
     )
 
     def sum_send(which, stage, tile):
-        base, count, me, peer = groups[stage]
+        base, count, me, peers = groups[stage]
         red[which, base + me] = tile
         at = red.at[which, base + me]
         for d in range(1, count):
-            remote(at, at, ar_s.at[which, stage], ar_r.at[which, stage], peer(d)).start()
+            remote(at, at, ar_s.at[which, stage], ar_r.at[which, stage], peers[d]).start()
 
     def sum_take(which, stage):
         base, count, _, _ = groups[stage]
@@ -174,7 +188,7 @@
         return out
 
     def own_block(i):
-        return span(own * wb + i * ROWS, ROWS)
+        return span(own + i * ROWS, ROWS)
 
     def accumulate(term):
         def trip(i, acc):
@@ -189,7 +203,7 @@
         sum_send(0, 0, narrow(acc))
 
     def alpha_close(slot):
-        value = jnp.full((ROWS, wa), jnp.sum(sum_take(0, 2)), jnp.float32)
+        value = jnp.full((ROWS, wa), jnp.sum(sum_take(0, 1)), jnp.float32)
         sc[0] = value
         scal_ref[slot] = value[:, :lanes]
 
@@ -204,7 +218,7 @@
         sum_send(1, 0, narrow(accumulate(term)))
 
     def beta_close(slot):
-        value = jnp.sqrt(jnp.full((ROWS, wa), jnp.sum(sum_take(1, 2)), jnp.float32))
+        value = jnp.sqrt(jnp.full((ROWS, wa), jnp.sum(sum_take(1, 1)), jnp.float32))
         sc[1] = value
         scal_ref[LANCZOS_STEPS + slot] = value[:, :lanes]
 
@@ -215,45 +229,50 @@
 
         fold(trip, wb // ROWS)
 
-    def r_rows(e, of_sub, q):
-        return rbuf.at[span((e // PIECES) * wb + of_sub * half + q * quart + (e % PIECES) * bit, bit), :]
-
-    q_own, q_mate = (x % 2) * 2 + c, (1 - x % 2) * 2 + c
-    q_sib, q_sib_mate = (x % 2) * 2 + 1 - c, (1 - x % 2) * 2 + 1 - c
+    def r_rows(e, of_sub, xx, cc):
+        start = (e // PIECES) * wb + of_sub * half + (xx * 2 + cc) * part + (e % PIECES) * bit
+        return rbuf.at[span(start, bit), :]
 
     def r_copy(way, e, gone):
-        sems = rr_s.at[way, e], rr_r.at[way, e]
         if way == 0:
-            src = r_hbm.at[e // PIECES, span(q_own * quart + (e % PIECES) * bit, bit), :]
-            return remote(src, r_rows(e, sub if gone else 1 - sub, q_own), *sems, yl_partner)
-        here, there = (q_mate, q_sib_mate) if way == 3 else (q_own, q_mate if way == 1 else q_sib)
-        at = r_rows(e, 1 - sub, here if gone else there)
-        return remote(at, at, *sems, x_mate if way == 1 else sibling)
-
-    def r_first(e):
-        r_copy(0, e, HERE).wait_recv()
-        r_copy(1, e, GONE).start()
-        r_copy(2, e, GONE).start()
-
-    def r_second(e):
-        r_copy(1, e, HERE).wait_recv()
-        r_copy(3, e, GONE).start()
+            src = r_hbm.at[e // PIECES, span(row * part + (e % PIECES) * bit, bit), :]
+            return remote(src, r_rows(e, sub if gone else 1 - sub, x, c), rr_s.at[0, e], rr_r.at[0, e], yl_partner)
+        over = isinstance(way, tuple)
+        from_way = way[0] if over else way
+        slot = from_way % 4
+        d = from_way if from_way in WAYS else 1 if e % PIECES == 0 else -1
+        away = {0: 0, 2: 2}.get(from_way, -d) - (d if gone and not over else 0)
+        away = -d if gone and not over and from_way == 2 else 0 if gone and not over else away
+        at = r_rows(e, 1 - sub, xs[away], 1 - c if over and not gone else c)
+        slot = slot + 4 if over else slot
+        return remote(at, at, rr_s.at[slot, e], rr_r.at[slot, e], sibling if over else x_next[d])
+
+    def r_take(way, e):
+        for d in WAYS if way == 1 else (way,):
+            r_copy(d, e, HERE).wait_recv()
+            r_copy((d,), e, GONE).start()
+            if way == 0:
+                for n in WAYS:
+                    r_copy(n, e, GONE).start()
+            elif way == 1 and d == (1 if e % PIECES == 0 else -1):
+                r_copy(2, e, GONE).start()
 
     def r_last():
         for e in range(3 * PIECES):
-            r_copy(2, e, HERE).wait_recv()
-            r_copy(3, e, HERE).wait_recv()
-            for way in range(4):
+            for way in (0, 1, -1, 2):
+                r_copy((way,), e, HERE).wait_recv()
+                r_copy((way,), e, GONE).wait_send()
                 r_copy(way, e, GONE).wait_send()
 
     def right_group(p, s, h, way):
         d = 1 if way == "+" else -1
         for q in range(s * SPLIT, s * SPLIT + SPLIT):
             for e in (d,) if way != "*" else WAYS if h else (0,):
-                pair_copy(p, q, 0, e, h, HERE).wait_recv()
+                if cut(q):
+                    pair_copy(p, q, 0, e, h, HERE).wait_recv()
 
         def one(i, carry):
-            start = pl.multiple_of((zat(-d * h) * 2 + i) * wb, wb)
+            start = pl.multiple_of((zs[-d * h] * 2 + i) * wb, wb)
             ubuf[s] = ubuf[s] + jnp.dot(
                 rbuf[:, pl.ds(start, wb)],
                 vbuf[p, s, pl.ds(start, wb), :],
@@ -271,20 +290,22 @@
 
         fold(trip, 3 * wb // ROWS)
 
-    def mix():
+    def mix(q):
+        t, base = q // SPLIT, (q % SPLIT) * mb
+
         def trip(i):
-            tiles = [[ubuf[s, span(r * wb + i * ROWS, ROWS), :] for s in PAIR] for r in TRIPLE]
-            for t in PAIR:
-                for l in TRIPLE:
-                    acc = None
-                    for r in TRIPLE:
-                        for s in PAIR:
-                            term = w_ref[((l * 3 + r) * 2 + s) * 2 + t] * tiles[r][s]
-                            acc = term if acc is None else acc + term
-                    tbuf[t, block(i), l * wa : (l + 1) * wa] = acc
-
-        fold(trip, wb // ROWS, 1)
-        clear_products()
+            tiles = [[ubuf[s, span(r * wb + base + i * ROWS, ROWS), :] for s in PAIR] for r in TRIPLE]
+            for l in TRIPLE:
+                acc = None
+                for r in TRIPLE:
+                    for s in PAIR:
+                        term = w_ref[((l * 3 + r) * 2 + s) * 2 + t] * tiles[r][s]
+                        acc = term if acc is None else acc + term
+                tbuf[t, span(base + i * ROWS, ROWS), l * wa : (l + 1) * wa] = acc
+
+        fold(trip, mb // ROWS, 1)
+        if q == chunks[-1]:
+            clear_products()
 
     def sib_copy(q, i):
         return remote(yb.at[i], rd.at[q, i], rd_s.at[i], rd_r.at[q, i], sibling)
@@ -292,9 +313,9 @@
     def left_products(q, part):
         def one(n, carry):
             theirs = n < (2, 2, 0)[part]
-            i = n % 2 if part == 0 else n + 3 - part
+            i = mod(n, 2) if part == 0 else n + 3 - part
             away = jnp.where(i < 2, i + 2, 3 - i)
-            start = (((x + away) % nx) * 2 + jnp.where(theirs, 1 - c, c)) * 2 * wa
+            start = (mod(x + away, nx) * 2 + jnp.where(theirs, 1 - c, c)) * 2 * wa
             yb[jnp.where(theirs, i, i + 4)] = jnp.dot(
                 tbuf[q // SPLIT, (q % SPLIT) * mb : (q % SPLIT + 1) * mb, :],
                 lbuf[:, pl.ds(pl.multiple_of(start, 2 * wa), 2 * wa)],
@@ -312,8 +333,10 @@
             sib_copy(q - 1, i).wait_send()
         lax.fori_loop(0, (3, 2, 3)[part], one, 0)
 
+    lane_at = {GONE: (1 - yl) * wa, HERE: yl * wa}
+
     def lane(theirs):
-        return pl.ds(pl.multiple_of((1 - yl if theirs else yl) * wa, wa), wa)
+        return pl.ds(pl.multiple_of(lane_at[theirs], wa), wa)
 
     def half_copy(p, q, d, theirs):
         slot, side = 0 if d > 0 else 1, 0 if theirs else 1
@@ -323,7 +346,8 @@
     def full_copy(p, q, d, theirs):
         slot, side = 0 if d > 0 else 1, 0 if theirs else 1
         src = rd.at[q, 2 - slot, :, lane(theirs)]
-        return remote(src, fx.at[p, q, slot, side], fx_s.at[q, slot, side], fx_r.at[p, q, slot, side], x_next[d])
+        to = (x_side if theirs else x_next)[d]
+        return remote(src, fx.at[p, q, slot, side], fx_s.at[q, slot, side], fx_r.at[p, q, slot, side], to)
 
     def cross_copy(p, q):
         return remote(rd.at[q, 3, :, lane(GONE)], yx.at[p, q], yx_s.at[q], yx_r.at[p, q], yl_partner)
@@ -352,24 +376,13 @@
 
             fold(add_half, mb // 2 // ROWS)
             full_copy(p, q, d, theirs).start()
-
-    def chip_sum(p, q, theirs):
-        lanes_at, side = lane(theirs), 0 if theirs else 1
-        for d in WAYS:
-            full_copy(p, q, d, theirs).wait_recv()
-
-        def add(k):
-            rows = block(k)
-            rd[q, 3, rows, lanes_at] = rd[q, 3, rows, lanes_at] + fx[p, q, 0, side, rows, :] + fx[p, q, 1, side, rows, :]
-
-        fold(add, mb // ROWS)
-
-    def open_cross(p, q):
-        chip_sum(p, q, GONE)
-        cross_copy(p, q).start()
+        else:
+            cross_copy(p, q).start()
 
     def close_chunk(p, q, more):
-        chip_sum(p, q, HERE)
+        for theirs in (GONE, HERE):
+            for d in WAYS:
+                full_copy(p, q, d, theirs).wait_recv()
         cross_copy(p, q).wait_recv()
         alpha, beta, old = sc[0], sc[1], sc[2]
         s, mine = q // SPLIT, lane(HERE)
@@ -377,6 +390,8 @@
         def step(k):
             rows, at = block(k), own_block(k + (q % SPLIT) * mb // ROWS)
             g = rd[q, 3, rows, mine] + yx[p, q, rows, :]
+            for slot in PAIR:
+                g = g + (fx[p, q, slot, 0, rows, :] + fx[p, q, slot, 1, rows, :])
             vbuf[1 - p, s, at, :] = (g - alpha * vbuf[p, s, at, :] - old * vbuf[1 - p, s, at, :]) / beta
 
         fold(step, mb // ROWS)
@@ -399,7 +414,7 @@
         return pltpu.make_async_copy(r_hbm.at[r], rbuf.at[span(r * wb + sub * half, half), :], ld_s.at[3 + r])
 
     def psi_at(s, of_sub):
-        return vbuf.at[0, s, span(own * wb + of_sub * half, half), :]
+        return vbuf.at[0, s, span(own + of_sub * half, half), :]
 
     def psi_load(s):
         return pltpu.make_async_copy(psi_ref.at[yl, s], psi_at(s, sub), ld_s.at[6 + s])
@@ -409,6 +424,12 @@
 
     for s in PAIR:
         psi_load(s).start()
+    barrier = pltpu.get_barrier_semaphore()
+    for _, count, _, peers in groups:
+        for d in range(1, count):
+            pl.semaphore_signal(barrier, inc=1, device_id=peers[d], device_id_type=MESH)
+    pl.semaphore_wait(barrier, plane + nz - 2)
+    for s in PAIR:
         psi_copy(s, GONE).start()
     for e in range(3 * PIECES):
         r_copy(0, e, GONE).start()
@@ -443,18 +464,17 @@
             return functools.partial(close_chunk, p, *args, more)
         if kind == "d":
             return functools.partial(drain_gather, p)
-        if kind == "l":
-            return functools.partial(left_products, *args)
-        return functools.partial({"p": take_pair, "h": take_hop, "f": left_sum, "o": open_cross}[kind], p, *args)
+        if kind in "lx":
+            return functools.partial({"l": left_products, "x": mix}[kind], *args)
+        return functools.partial({"p": take_pair, "h": take_hop, "f": left_sum}[kind], p, *args)
 
     gather_order = ",".join(GATHER_ORDER).split(",")
     reduce_order = ",".join(REDUCE_ORDER).split(",")
     r_plan = []
-    for e in range(3 * PIECES + 2):
-        if e < 3 * PIECES:
-            r_plan.append(functools.partial(r_first, e))
-        if e > 1:
-            r_plan.append(functools.partial(r_second, e - 2))
+    for e in range(3 * PIECES + 4):
+        for way in TRIPLE:
+            if 0 <= e - 2 * way < 3 * PIECES:
+                r_plan.append(functools.partial(r_take, way, e - 2 * way))
 
     for s in PAIR:
         psi_load(s).wait()
@@ -466,7 +486,7 @@
             work(name, 0, None, None)()
         elif int(name[1]) % SPLIT:
             own_sends(0, int(name[1]))
-        if n % 3 > 0 and n * 3 > len(served):
+        if n % 2 == 0 and n * 3 > len(served):
             r_plan.pop(0)()
     for r in TRIPLE:
         r_load(r).wait()
@@ -475,8 +495,8 @@
         psi_copy(s, GONE).wait_send()
 
     def lanczos_step(j, carry):
-        p = j % 2
-        slot = (j + LANCZOS_STEPS - 1) % LANCZOS_STEPS
+        p = mod(j, 2)
+        slot = mod(j + LANCZOS_STEPS - 1, LANCZOS_STEPS)
         more = j < LANCZOS_STEPS - 1
 
         rest = list(r_plan)
@@ -493,7 +513,7 @@
 
                 rest = None if name[0] == "m" else rest
             work(name, p, more, slot)()
-        mix()
+        mix(0)
 
         pl.semaphore_wait(credit, 1)
         for name in reduce_order:
@@ -523,13 +543,11 @@
 
     alpha_open(p)
     sum_pass(0, 1)
-    sum_pass(0, 2)
     alpha_close(LANCZOS_STEPS - 1)
     beta_open(p)
     for s in PAIR:
         out_copy(s).start()
     sum_pass(1, 1)
-    sum_pass(1, 2)
     beta_close(LANCZOS_STEPS - 1)
     for s in PAIR:
         out_copy(s).wait_recv()
@@ -584,7 +602,7 @@
                 vmem((2, parts, 2, 2, mb, wa), f32),
                 vmem((2, parts, mb, wa), f32),
                 vmem((2, half, wa), f32),
-                vmem((2, nx * 2 + 4 + nz, ROWS, lanes), f32),
+                vmem((2, nx * 8 + nz, ROWS, lanes), f32),
                 vmem((3, ROWS, wa), f32),
                 dma((parts, ids)),
                 dma((2, parts, ids)),
@@ -596,16 +614,16 @@
                 dma((2, parts, 2, 2)),
                 dma((parts,)),
                 dma((2, parts)),
-                dma((2, 3)),
-                dma((2, 3)),
-                dma((4, 3 * PIECES)),
-                dma((4, 3 * PIECES)),
+                dma((2, 2)),
+                dma((2, 2)),
+                dma((8, 3 * PIECES)),
+                dma((8, 3 * PIECES)),
                 dma((4,)),
                 dma((4,)),
                 dma((8,)),
                 pltpu.SemaphoreType.REGULAR,
             ],
-            compiler_params=pltpu.CompilerParams(has_side_effects=True, vmem_limit_bytes=66 * 1000 * 1000),
+            compiler_params=pltpu.CompilerParams(collective_id=0, has_side_effects=True, vmem_limit_bytes=66 * 1000 * 1000),
             name="lanczos",
         )(psi_t, jnp.transpose(left_blk, (1, 0, 2)), mpo_tensor.reshape(-1), jnp.transpose(right_blk, (1, 0, 2)))
         v_next = jnp.transpose(v_out, (0, 3, 1, 2)).reshape(psi_blk.shape)

time: 463 us -> 434 us (0.937)
  Pallas kernels: 455 us -> 426 us
    pallas_call x1, Pallas kernels: 455 us -> 426 us  [local_steps(): pl.pallas_call(kernel, out_shape=(jax.ShapeDtypeStruct((2 * LANCZOS_STEPS...]
where the time goes in v3:
time: 434 us
  Pallas kernels  426 us (98%)
  local copies, waits for them, and re-layouts  7.25 us (2%)
    pallas_call x1, Pallas kernels, local_steps(): pl.pallas_call(kernel, out_shape=(jax.ShapeDtypeStruct((2 * LANCZOS_STEPS...  426 us

profile of v3, /device:TPU:1, one launch (start us, length us, event | category | flops | bytes accessed | tf_op | source)
XLA Modules:
  0.0 433.6 jit_solution(7621639216724377388)
XLA Ops:
  0.6 0.8 copy.10
  1.4 0.6 reshape.16.w_ref
  2.0 2.0 copy.9
  4.1 425.7 %lanczos.1 = (f32[8,8,128]{2,1,0:T(8,128)}, f32[2,2,128,256]{3,2,1,0:T(8,128)}) custom-call(f32[2,2,128,256]{3,2,1,0:T(8,128)} %bitcast.8, f32[3,512,4096]{2,1,0:T(8,128)} %bitcast.6, f32[36]{0:T(128)} %reshape.16.w_ref, f32[3,128,4096]{2,1,0:T(8,128)} %bitcast.7), custom_call_target="tpu_custom_call" | custom-call | tf_op jit(solution)/shard_map/lanczos/pallas_call | solution.py:579
  429.8 1.4 slice_reduce_fusion
  431.2 1.2 copy.11
  432.4 1.2 copy.12

commit v4 on v3

--- a/solution.py
+++ b/solution.py
@@ -13,19 +13,24 @@
 ROWS = 8
 SPLIT = 2
 PIECES = 2
+START_ORDER = (
+    "h001,r00,p0,h011,c1,h021,h002,r01,r02,r10,h101,p1,r03,h022",
+    "r11,h121,h012,r04,h023,h102,h013,c3,r05,r20,r12,r13,r21,h111",
+    "h122,h003,h112,r14,r15,h201,r22,h113,p2,h211",
+)
 GATHER_ORDER = (
-    "a0,h103,p2,h113,h123,h202,h212,h301,h311,m00*,h104,h221,m01+",
-    "h114,h124,m01-,h203,p3,h213,m02+,h302,m02-,h312,a1,m03+,h222",
-    "h204,m03-,h321,m10*,h214,h303,m11+,h313,m11-,h223,m04*,h322",
-    "b0,h304,m12+,h314,h224,m12-,h323,m13+,m13-,h324,b1,m14*",
+    "h004,h114,r23,h014,h123,r24,r25,a0,h301,h103,w,h202,h024",
+    "m02+,h221,m02-,p3,m01+,h311,h104,h212,h302,m00*,h203,m01-",
+    "m10*,h222,m03+,a1,h321,h124,m11+,h303,h312,m03-,h223,m11-",
+    "h322,m04*,h204,h304,b0,m12+,h213,h313,h224,m12-,h323,m13-",
+    "m13+,h314,h214,b1,h324,m14*",
 )
 REDUCE_ORDER = (
-    "l00,f000,l01,l02,f030,f010,f020,x1,d0,b3,f011,f021,l10,f100",
-    "l11,l12,f130,x2,l20,c0,f110,f120,f111,f121,f200,l21,l22,p0",
-    "h001,h011,f230,x3,l30,h021,c1,f300,l31,h002,h012,f210,f220",
-    "f211,f221,h022,l32,p1,h101,h111,f330,f310,f320,f311,f321",
-    "h003,h013,h023,h121,c2,h102,h112,h004,h014,h024,h122,h201",
-    "h211,c3",
+    "d0,l00,f000,x2,x1,l01,f030,l02,f020,b3,f010,f011,l10,f021",
+    "l11,f100,l12,f130,l20,f120,c0,f110,l21,p0,f121,f111,x3,f200",
+    "h001,l22,h011,h021,l30,f300,f230,c1,h002,f220,f210,l31,p1",
+    "h111,f211,h012,f221,l32,f320,h101,f310,h022,f311,h003,h112",
+    "f330,h121,c2,f321,h122,h013,h113,h102,h023,h211,p2,h201,c3",
 )
 PAIR = range(2)
 TRIPLE = range(3)
@@ -299,7 +304,7 @@
                 acc = None
                 for r in TRIPLE:
                     for s in PAIR:
-                        term = w_ref[((l * 3 + r) * 2 + s) * 2 + t] * tiles[r][s]
+                        term = w_ref[l, s, t, r] * tiles[r][s]
                         acc = term if acc is None else acc + term
                 tbuf[t, span(base + i * ROWS, ROWS), l * wa : (l + 1) * wa] = acc
 
@@ -312,8 +317,8 @@
 
     def left_products(q, part):
         def one(n, carry):
-            theirs = n < (2, 2, 0)[part]
-            i = mod(n, 2) if part == 0 else n + 3 - part
+            theirs = (n < 2, n > 0, n < 0)[part]
+            i = n + 1 if part == 2 else jnp.where(n == 1 - part, 3, n * part)
             away = jnp.where(i < 2, i + 2, 3 - i)
             start = (mod(x + away, nx) * 2 + jnp.where(theirs, 1 - c, c)) * 2 * wa
             yb[jnp.where(theirs, i, i + 4)] = jnp.dot(
@@ -329,9 +334,9 @@
 
             return carry
 
-        for i in ((0, 1), (2, 3), ())[part] if q else ():
+        for i in ((0, 3), (1, 2), ())[part] if q else ():
             sib_copy(q - 1, i).wait_send()
-        lax.fori_loop(0, (3, 2, 3)[part], one, 0)
+        lax.fori_loop(0, (3, 3, 2)[part], one, 0)
 
     lane_at = {GONE: (1 - yl) * wa, HERE: yl * wa}
 
@@ -464,30 +469,26 @@
             return functools.partial(close_chunk, p, *args, more)
         if kind == "d":
             return functools.partial(drain_gather, p)
+        if kind == "w":
+            return r_last
+        if kind == "r":
+            return functools.partial(r_take, *args)
         if kind in "lx":
             return functools.partial({"l": left_products, "x": mix}[kind], *args)
         return functools.partial({"p": take_pair, "h": take_hop, "f": left_sum}[kind], p, *args)
 
-    gather_order = ",".join(GATHER_ORDER).split(",")
-    reduce_order = ",".join(REDUCE_ORDER).split(",")
-    r_plan = []
-    for e in range(3 * PIECES + 4):
-        for way in TRIPLE:
-            if 0 <= e - 2 * way < 3 * PIECES:
-                r_plan.append(functools.partial(r_take, way, e - 2 * way))
-
+    start_order, gather_order, reduce_order = (
+        ",".join(order).split(",") for order in (START_ORDER, GATHER_ORDER, REDUCE_ORDER)
+    )
     for s in PAIR:
         psi_load(s).wait()
         psi_copy(s, HERE).wait_recv()
         own_sends(0, s * SPLIT)
-    served = [name for name in reduce_order if name[0] in "phc"]
-    for n, name in enumerate(served):
-        if name[0] != "c":
+    for name in start_order:
+        if name[0] == "c":
+            own_sends(0, int(name[1]))
+        else:
             work(name, 0, None, None)()
-        elif int(name[1]) % SPLIT:
-            own_sends(0, int(name[1]))
-        if n % 2 == 0 and n * 3 > len(served):
-            r_plan.pop(0)()
     for r in TRIPLE:
         r_load(r).wait()
         l_load(r).wait()
@@ -499,20 +500,11 @@
         slot = mod(j + LANCZOS_STEPS - 1, LANCZOS_STEPS)
         more = j < LANCZOS_STEPS - 1
 
-        rest = list(r_plan)
         for name in gather_order:
-            if name[0] == "m" and rest is not None or name[0] in "ph" and rest:
-                now = len(rest) if name[0] == "m" else 2
-
-                @pl.when(j == 0)
-                def _():
-                    for _ in range(min(now, len(rest))):
-                        rest.pop(0)()
-                    if name[0] == "m":
-                        r_last()
-
-                rest = None if name[0] == "m" else rest
-            work(name, p, more, slot)()
+            if name[0] in "rw":
+                pl.when(j == 0)(work(name, p, more, slot))
+            else:
+                work(name, p, more, slot)()
         mix(0)
 
         pl.semaphore_wait(credit, 1)
@@ -625,7 +617,7 @@
             ],
             compiler_params=pltpu.CompilerParams(collective_id=0, has_side_effects=True, vmem_limit_bytes=66 * 1000 * 1000),
             name="lanczos",
-        )(psi_t, jnp.transpose(left_blk, (1, 0, 2)), mpo_tensor.reshape(-1), jnp.transpose(right_blk, (1, 0, 2)))
+        )(psi_t, jnp.transpose(left_blk, (1, 0, 2)), jnp.transpose(mpo_tensor, (0, 2, 3, 1)), jnp.transpose(right_blk, (1, 0, 2)))
         v_next = jnp.transpose(v_out, (0, 3, 1, 2)).reshape(psi_blk.shape)
         return scalars[:LANCZOS_STEPS, 0, 0], scalars[LANCZOS_STEPS:, 0, 0], v_next
 

time: 434 us -> 429 us (0.988)
  no operation moved by 1% of the time
where the time goes in v4:
time: 429 us
  Pallas kernels  422 us (98%)
  local copies, waits for them, and re-layouts  5.84 us (1%)
    pallas_call x1, Pallas kernels, local_steps(): pl.pallas_call(kernel, out_shape=(jax.ShapeDtypeStruct((2 * LANCZOS_STEPS...  422 us

profile of v4, /device:TPU:1, one launch (start us, length us, event | category | flops | bytes accessed | tf_op | source)
XLA Modules:
  0.0 428.9 jit_solution(6415310660230188061)
XLA Ops:
  0.6 2.0 copy.8
  2.7 422.4 %lanczos.1 = (f32[8,8,128]{2,1,0:T(8,128)}, f32[2,2,128,256]{3,2,1,0:T(8,128)}) custom-call(f32[2,2,128,256]{3,2,1,0:T(8,128)} %bitcast.9, f32[3,512,4096]{2,1,0:T(8,128)} %bitcast.7, f32[3,2,2,3]{3,2,1,0:T(2,128)} %bitcast.13, f32[3,128,4096]{2,1,0:T(8,128)} %bitcast.8), custom_call_target="tpu_custom_call" | custom-call | tf_op jit(solution)/shard_map/lanczos/pallas_call | solution.py:571
  425.1 1.4 slice_reduce_fusion
  426.5 1.2 copy.9
  427.7 1.2 copy.10

commit v5 on v4

--- a/solution.py
+++ b/solution.py
@@ -14,23 +14,24 @@
 SPLIT = 2
 PIECES = 2
 START_ORDER = (
-    "h001,r00,p0,h011,c1,h021,h002,r01,r02,r10,h101,p1,r03,h022",
-    "r11,h121,h012,r04,h023,h102,h013,c3,r05,r20,r12,r13,r21,h111",
-    "h122,h003,h112,r14,r15,h201,r22,h113,p2,h211",
+    "p0,c1,r00,r01,h001,r02,h011,h111,h101,p1,r03,r11,h012,h201",
+    "r10,r05,r04,c3,h021,h121,h102,h002,r15,r12,p2,h112,h022,h211",
+    "r13,r21,r14,h003,r22,h301,r20,h122,h023,r24,h013,h113,h103",
 )
 GATHER_ORDER = (
-    "h004,h114,r23,h014,h123,r24,r25,a0,h301,h103,w,h202,h024",
-    "m02+,h221,m02-,p3,m01+,h311,h104,h212,h302,m00*,h203,m01-",
-    "m10*,h222,m03+,a1,h321,h124,m11+,h303,h312,m03-,h223,m11-",
-    "h322,m04*,h204,h304,b0,m12+,h213,h313,h224,m12-,h323,m13-",
-    "m13+,h314,h214,b1,h324,m14*",
+    "a0,r23,p3,h311,r25,w,m01+,m02-,m02+,h221,h302,h202,h123,h024",
+    "m01-,h104,m10*,h004,h114,h321,m00*,h212,m03-,a1,h222,m11+",
+    "h303,h312,m11-,h322,m03+,h203,h213,m12-,b0,h014,h124,h223",
+    "m04*,h304,h313,m12+,h323,h204,m13+,m13-,h214,h324,b1,h224",
+    "h314,m14*",
 )
 REDUCE_ORDER = (
-    "d0,l00,f000,x2,x1,l01,f030,l02,f020,b3,f010,f011,l10,f021",
-    "l11,f100,l12,f130,l20,f120,c0,f110,l21,p0,f121,f111,x3,f200",
-    "h001,l22,h011,h021,l30,f300,f230,c1,h002,f220,f210,l31,p1",
-    "h111,f211,h012,f221,l32,f320,h101,f310,h022,f311,h003,h112",
-    "f330,h121,c2,f321,h122,h013,h113,h102,h023,h211,p2,h201,c3",
+    "x1,l00,f000,l01,f030,l02,f010,f020,l10,f100,l11,f011,f021",
+    "l12,f130,x2,f120,f110,l20,d0,b3,c0,f200,f121,f111,l21,f230",
+    "l22,f220,f210,p0,x3,h001,h011,l30,c1,f300,l31,f330,h021,f221",
+    "f211,h002,p1,h101,l32,h111,f320,f310,h012,f311,h022,f321,c2",
+    "h112,h102,h003,h121,c3,h201,h122,h013,h103,h113,h023,h301",
+    "h211,p2",
 )
 PAIR = range(2)
 TRIPLE = range(3)

time: 429 us -> 418 us (0.974)
  Pallas kernels: 422 us -> 412 us
    pallas_call x1, Pallas kernels: 422 us -> 412 us  [local_steps(): pl.pallas_call(kernel, out_shape=(jax.ShapeDtypeStruct((2 * LANCZOS_STEPS...]
where the time goes in v5:
time: 418 us
  Pallas kernels  412 us (99%)
  local copies, waits for them, and re-layouts  5.84 us (1%)
    pallas_call x1, Pallas kernels, local_steps(): pl.pallas_call(kernel, out_shape=(jax.ShapeDtypeStruct((2 * LANCZOS_STEPS...  412 us

profile of v5, /device:TPU:1, one launch (start us, length us, event | category | flops | bytes accessed | tf_op | source)
XLA Modules:
  0.0 418.0 jit_solution(12214685164441732001)
XLA Ops:
  0.6 2.0 copy.8
  2.7 411.5 %lanczos.1 = (f32[8,8,128]{2,1,0:T(8,128)}, f32[2,2,128,256]{3,2,1,0:T(8,128)}) custom-call(f32[2,2,128,256]{3,2,1,0:T(8,128)} %bitcast.9, f32[3,512,4096]{2,1,0:T(8,128)} %bitcast.7, f32[3,2,2,3]{3,2,1,0:T(2,128)} %bitcast.13, f32[3,128,4096]{2,1,0:T(8,128)} %bitcast.8), custom_call_target="tpu_custom_call" | custom-call | tf_op jit(solution)/shard_map/lanczos/pallas_call | solution.py:572
  414.2 1.4 slice_reduce_fusion
  415.6 1.2 copy.9
  416.8 1.2 copy.10

commit v6 on v4

--- a/solution.py
+++ b/solution.py
@@ -14,23 +14,24 @@
 SPLIT = 2
 PIECES = 2
 START_ORDER = (
-    "h001,r00,p0,h011,c1,h021,h002,r01,r02,r10,h101,p1,r03,h022",
-    "r11,h121,h012,r04,h023,h102,h013,c3,r05,r20,r12,r13,r21,h111",
-    "h122,h003,h112,r14,r15,h201,r22,h113,p2,h211",
+    "r00,c1,r01,p1,r02,p0,h111,h001,r03,h011,r11,h121,h101,r10",
+    "h012,h021,r05,h002,h102,r20,c3,r04,r15,r21,r13,p2,h022,r12",
+    "h201,r14,h103,h112",
 )
 GATHER_ORDER = (
-    "h004,h114,r23,h014,h123,r24,r25,a0,h301,h103,w,h202,h024",
-    "m02+,h221,m02-,p3,m01+,h311,h104,h212,h302,m00*,h203,m01-",
-    "m10*,h222,m03+,a1,h321,h124,m11+,h303,h312,m03-,h223,m11-",
-    "h322,m04*,h204,h304,b0,m12+,h213,h313,h224,m12-,h323,m13-",
-    "m13+,h314,h214,b1,h324,m14*",
+    "n00*,r25,h122,h023,h301,h013,p3,a0,r24,r22,h003,r23,w,k01-",
+    "h221,n02+,h211,k02-,m10*,h302,h311,h202,n02-,n01-,h123,h113",
+    "h104,k01+,h321,n01+,h212,m03+,m11-,k02+,a1,m03-,h303,h312",
+    "m11+,h114,k00*,h004,h024,h222,h322,h203,m12-,m12+,h014,h213",
+    "b0,h223,h124,h313,m04*,h323,h304,h204,m13-,b1,h214,m13+,h324",
+    "h224,h314,m14*",
 )
 REDUCE_ORDER = (
-    "d0,l00,f000,x2,x1,l01,f030,l02,f020,b3,f010,f011,l10,f021",
-    "l11,f100,l12,f130,l20,f120,c0,f110,l21,p0,f121,f111,x3,f200",
-    "h001,l22,h011,h021,l30,f300,f230,c1,h002,f220,f210,l31,p1",
-    "h111,f211,h012,f221,l32,f320,h101,f310,h022,f311,h003,h112",
-    "f330,h121,c2,f321,h122,h013,h113,h102,h023,h211,p2,h201,c3",
+    "l00,x1,b3,f000,l01,f030,l02,f010,f020,l10,f021,x2,f100,l11",
+    "f130,f011,l12,d0,f110,f120,l20,f121,f111,c0,f200,l21,p0,f230",
+    "l22,x3,h001,c1,h011,f210,f220,h021,l30,f211,f300,h002,l31",
+    "f330,f221,h101,h012,h022,l32,h111,f320,f310,f311,f321,p1,c2",
+    "h102,h121,h112,p2,c3,h201,h103",
 )
 PAIR = range(2)
 TRIPLE = range(3)
@@ -455,7 +456,7 @@
     sc[2] = jnp.zeros((ROWS, wa), jnp.float32)
     def work(name, p, more, slot):
         kind, tail = name[0], name[1:]
-        if kind == "m":
+        if kind in "mnk":
             return functools.partial(right_group, p, int(tail[0]), int(tail[1]), tail[2])
         args = [int(digit) for digit in tail]
         if kind in "ab":
@@ -501,8 +502,10 @@
         more = j < LANCZOS_STEPS - 1
 
         for name in gather_order:
-            if name[0] in "rw":
+            if name[0] in "rwk":
                 pl.when(j == 0)(work(name, p, more, slot))
+            elif name[0] == "n":
+                pl.when(j > 0)(work(name, p, more, slot))
             else:
                 work(name, p, more, slot)()
         mix(0)

time: 429 us -> 428 us (level)
  no operation moved by 1% of the time
where the time goes in v6:
time: 428 us
  Pallas kernels  421 us (98%)
  local copies, waits for them, and re-layouts  5.84 us (1%)
    pallas_call x1, Pallas kernels, local_steps(): pl.pallas_call(kernel, out_shape=(jax.ShapeDtypeStruct((2 * LANCZOS_STEPS...  421 us

profile of v6, /device:TPU:1, one launch (start us, length us, event | category | flops | bytes accessed | tf_op | source)
XLA Modules:
  0.0 427.6 jit_solution(6859636388715981991)
XLA Ops:
  0.6 2.0 copy.8
  2.7 421.1 %lanczos.1 = (f32[8,8,128]{2,1,0:T(8,128)}, f32[2,2,128,256]{3,2,1,0:T(8,128)}) custom-call(f32[2,2,128,256]{3,2,1,0:T(8,128)} %bitcast.9, f32[3,512,4096]{2,1,0:T(8,128)} %bitcast.7, f32[3,2,2,3]{3,2,1,0:T(2,128)} %bitcast.13, f32[3,128,4096]{2,1,0:T(8,128)} %bitcast.8), custom_call_target="tpu_custom_call" | custom-call | tf_op jit(solution)/shard_map/lanczos/pallas_call | solution.py:574
  423.8 1.4 slice_reduce_fusion
  425.2 1.2 copy.9
  426.4 1.2 copy.10

commit v7 on v6

--- a/solution.py
+++ b/solution.py
@@ -14,24 +14,24 @@
 SPLIT = 2
 PIECES = 2
 START_ORDER = (
-    "r00,c1,r01,p1,r02,p0,h111,h001,r03,h011,r11,h121,h101,r10",
-    "h012,h021,r05,h002,h102,r20,c3,r04,r15,r21,r13,p2,h022,r12",
-    "h201,r14,h103,h112",
+    "p0,c1,h001,r00,r01,h011,r02,h101,h021,r10,p1,h111,c3,r03",
+    "h012,h102,r11,r05,h301,r04,r12,h211,h002,r15,h022,h121,r20",
+    "h112,h201,r14,p2,r13,h122",
 )
 GATHER_ORDER = (
-    "n00*,r25,h122,h023,h301,h013,p3,a0,r24,r22,h003,r23,w,k01-",
-    "h221,n02+,h211,k02-,m10*,h302,h311,h202,n02-,n01-,h123,h113",
-    "h104,k01+,h321,n01+,h212,m03+,m11-,k02+,a1,m03-,h303,h312",
-    "m11+,h114,k00*,h004,h024,h222,h322,h203,m12-,m12+,h014,h213",
-    "b0,h223,h124,h313,m04*,h323,h304,h204,m13-,b1,h214,m13+,h324",
-    "h224,h314,m14*",
+    "n02+,h311,a0,r25,r21,h103,n02-,n01+,r22,h113,r24,h023,h013",
+    "h212,h003,r23,w,p3,m10*,k01+,k01-,h202,n00*,h221,h114,h024",
+    "h104,k02-,a1,k02+,h123,h302,h321,m03-,h312,k00*,n01-,m11-",
+    "h303,h004,h222,h203,m03+,h322,m12-,h124,b0,m11+,h223,h313",
+    "h304,h213,h014,h204,m04*,h323,m13+,m12+,m13-,h324,h224,h314",
+    "h214,m14*,b1",
 )
 REDUCE_ORDER = (
-    "l00,x1,b3,f000,l01,f030,l02,f010,f020,l10,f021,x2,f100,l11",
-    "f130,f011,l12,d0,f110,f120,l20,f121,f111,c0,f200,l21,p0,f230",
-    "l22,x3,h001,c1,h011,f210,f220,h021,l30,f211,f300,h002,l31",
-    "f330,f221,h101,h012,h022,l32,h111,f320,f310,f311,f321,p1,c2",
-    "h102,h121,h112,p2,c3,h201,h103",
+    "x1,l00,f000,l01,l02,f020,f010,d0,x2,l10,f030,f100,f021,l11",
+    "f130,f011,l12,f110,f120,b3,l20,f200,c0,f111,l21,f230,f121",
+    "l22,p0,f210,f220,h001,f211,x3,h011,l30,h021,f300,f221,c1,l31",
+    "h002,f330,l32,f320,h022,p1,h012,f321,h101,h111,f310,h121,c2",
+    "f311,h102,h112,c3,h211,h301,h122,p2,h201",
 )
 PAIR = range(2)
 TRIPLE = range(3)

time: 428 us -> 426 us (level)
  no operation moved by 1% of the time
where the time goes in v7:
time: 426 us
  Pallas kernels  419 us (98%)
  local copies, waits for them, and re-layouts  5.84 us (1%)
    pallas_call x1, Pallas kernels, local_steps(): pl.pallas_call(kernel, out_shape=(jax.ShapeDtypeStruct((2 * LANCZOS_STEPS...  419 us

profile of v7, /device:TPU:1, one launch (start us, length us, event | category | flops | bytes accessed | tf_op | source)
XLA Modules:
  0.0 425.6 jit_solution(10090877939510169880)
XLA Ops:
  0.6 2.0 copy.8
  2.7 419.2 %lanczos.1 = (f32[8,8,128]{2,1,0:T(8,128)}, f32[2,2,128,256]{3,2,1,0:T(8,128)}) custom-call(f32[2,2,128,256]{3,2,1,0:T(8,128)} %bitcast.9, f32[3,512,4096]{2,1,0:T(8,128)} %bitcast.7, f32[3,2,2,3]{3,2,1,0:T(2,128)} %bitcast.13, f32[3,128,4096]{2,1,0:T(8,128)} %bitcast.8), custom_call_target="tpu_custom_call" | custom-call | tf_op jit(solution)/shard_map/lanczos/pallas_call | solution.py:574
  421.8 1.4 slice_reduce_fusion
  423.2 1.2 copy.9
  424.4 1.2 copy.10

commit v8 on v4

--- a/solution.py
+++ b/solution.py
@@ -14,23 +14,23 @@
 SPLIT = 2
 PIECES = 2
 START_ORDER = (
-    "h001,r00,p0,h011,c1,h021,h002,r01,r02,r10,h101,p1,r03,h022",
-    "r11,h121,h012,r04,h023,h102,h013,c3,r05,r20,r12,r13,r21,h111",
-    "h122,h003,h112,r14,r15,h201,r22,h113,p2,h211",
+    "r00,c1,r01,h011,h001,r02,p0,h101,r10,r11,h012,c3,p1,r03,h021",
+    "h002,r05,r04,h102,h111,h121,h022,r12,r15,h003,r20,p2,r21",
+    "h112,r13,r14,h113,r22,h013,h103,r24,r25,h023,h211,r23",
 )
 GATHER_ORDER = (
-    "h004,h114,r23,h014,h123,r24,r25,a0,h301,h103,w,h202,h024",
-    "m02+,h221,m02-,p3,m01+,h311,h104,h212,h302,m00*,h203,m01-",
-    "m10*,h222,m03+,a1,h321,h124,m11+,h303,h312,m03-,h223,m11-",
-    "h322,m04*,h204,h304,b0,m12+,h213,h313,h224,m12-,h323,m13-",
-    "m13+,h314,h214,b1,h324,m14*",
+    "a0,h301,h122,h201,p3,h221,h311,w,m00*,m10*,m01-,h302,m02+",
+    "m02-,h123,h024,h014,m01+,h202,h321,m03-,m03+,a1,h212,h222",
+    "h303,m11+,h104,h312,m11-,h322,h004,m12-,h203,h124,h213,m12+",
+    "h223,h114,b0,h304,h313,m04*,h323,h204,m13-,m13+,h214,h314",
+    "h224,h324,m14*,b1",
 )
 REDUCE_ORDER = (
-    "d0,l00,f000,x2,x1,l01,f030,l02,f020,b3,f010,f011,l10,f021",
-    "l11,f100,l12,f130,l20,f120,c0,f110,l21,p0,f121,f111,x3,f200",
-    "h001,l22,h011,h021,l30,f300,f230,c1,h002,f220,f210,l31,p1",
-    "h111,f211,h012,f221,l32,f320,h101,f310,h022,f311,h003,h112",
-    "f330,h121,c2,f321,h122,h013,h113,h102,h023,h211,p2,h201,c3",
+    "l00,x1,f000,l01,f030,l02,f010,f020,l10,x2,b3,f100,l11,f011",
+    "f021,f130,l12,f110,f120,l20,d0,c0,f200,f111,l21,p0,f230,f121",
+    "l22,h001,x3,f210,f220,h011,l30,h021,f211,c1,f221,h002,f300",
+    "p1,l31,h101,f330,l32,h111,f320,c2,h121,f310,f321,h102,f311",
+    "h112,p2,h012,h022,c3,h103,h023,h211,h013,h113,h003",
 )
 PAIR = range(2)
 TRIPLE = range(3)

time: 429 us -> 419 us (0.977)
  Pallas kernels: 422 us -> 412 us
    pallas_call x1, Pallas kernels: 422 us -> 412 us  [local_steps(): pl.pallas_call(kernel, out_shape=(jax.ShapeDtypeStruct((2 * LANCZOS_STEPS...]
where the time goes in v8:
time: 419 us
  Pallas kernels  412 us (98%)
  local copies, waits for them, and re-layouts  5.84 us (1%)
    pallas_call x1, Pallas kernels, local_steps(): pl.pallas_call(kernel, out_shape=(jax.ShapeDtypeStruct((2 * LANCZOS_STEPS...  412 us

profile of v8, /device:TPU:1, one launch (start us, length us, event | category | flops | bytes accessed | tf_op | source)
XLA Modules:
  0.0 418.7 jit_solution(7572241988775050432)
XLA Ops:
  0.6 2.0 copy.8
  2.7 412.2 %lanczos.1 = (f32[8,8,128]{2,1,0:T(8,128)}, f32[2,2,128,256]{3,2,1,0:T(8,128)}) custom-call(f32[2,2,128,256]{3,2,1,0:T(8,128)} %bitcast.9, f32[3,512,4096]{2,1,0:T(8,128)} %bitcast.7, f32[3,2,2,3]{3,2,1,0:T(2,128)} %bitcast.13, f32[3,128,4096]{2,1,0:T(8,128)} %bitcast.8), custom_call_target="tpu_custom_call" | custom-call | tf_op jit(solution)/shard_map/lanczos/pallas_call | solution.py:571
  414.9 1.4 slice_reduce_fusion
  416.2 1.2 copy.9
  417.5 1.2 copy.10
